TPU v7x, 32 devices: a whole 2x2x4 slice. The times are simulated.
32 devices in a mesh: dp: 16 (over z, y, x), tp: 2 (over core).
Axes of the slice: x: 2, y: 2, z: 4, core: 2. Of those that a mesh axis runs over, the one named last changes fastest.
Arguments:
- tokens: bfloat16 [2048, 4096], P('dp', 'tp'), may hold values from -6 to 6
- norm_gain: float32 [4096], replicated, may hold values from 0.1 to 1.9
- w_query: bfloat16 [4096, 2048], P(None, 'tp'), may hold values from -0.09375 to 0.09375
- w_key: bfloat16 [4096, 512], P(None, 'tp'), may hold values from -0.09375 to 0.09375
- w_value: bfloat16 [4096, 512], P(None, 'tp'), may hold values from -0.09375 to 0.09375
- w_out: bfloat16 [2048, 4096], P('tp'), may hold values from -0.125 to 0.125
- mlp_gain: float32 [4096], replicated, may hold values from 0.1 to 1.9
- w_gate: bfloat16 [4096, 7168], P(None, 'tp'), may hold values from -0.09375 to 0.09375
- w_up: bfloat16 [4096, 7168], P(None, 'tp'), may hold values from -0.09375 to 0.09375
- w_down: bfloat16 [7168, 4096], P('tp'), may hold values from -0.0625 to 0.0625
- kv_pool: bfloat16 [1024, 2, 4, 128, 128], P('dp', None, 'tp'), may hold values from -160 to 160, as said below
- prefix_len: int32 [16], replicated, may hold values from 1024 to 8192, as said below
- page_owner: int32 [16, 64], replicated, may hold values from -1 to 15, as said below
- page_slot: int32 [16, 64], replicated, may hold values from -1 to 63, as said below
- serving: int32 [16], replicated, may hold values from 0 to 15, each once
Outputs:
- context: bfloat16 [2048, 2048], P('dp', 'tp')
- layer_out: bfloat16 [2048, 4096], P('dp', 'tp')
Inputs may be any that keep to these rules, and one draw needn't show every extreme that they name: `prefix_len`: prefix lengths lie between 1024 and 8192; some request has exactly 8192 cached tokens and some exactly 1024. page_owner[r, p] names an index along dp for p < ceil(prefix_len[r] / 128) and is -1 after; no index holds more than 4 pages of one request, and for every request some index holds exactly 4 of its pages. page_slot[r, p] lies in 0 to 63 where page_owner[r, p] is not -1 and is -1 where it is; no two pages share the same holder and slot. serving is a permutation of the requests. `kv_pool`: cached keys and values, each page with an offset of its own.
All inputs are finite; a program needn't handle non-finite values.
Results may differ from a plain program's by a relative error of at most 0.014.
The roundings to bfloat16 on the way count: a program that leaves them out, or rounds other values in their place, can miss the bound.
Values may be sent and summed in bfloat16 or wider, within the bound.
A program may use at most 256 MiB of HBM per device.

v0:
```python
import functools
import math

import jax
import jax.numpy as jnp
from jax import lax
from jax.experimental import pallas as pl
from jax.experimental.pallas import tpu as pltpu
from jax.sharding import PartitionSpec as P

EPS = 1e-05
THETA = 500000.0
NEG = -1e30
MESH = pl.DeviceIdType.MESH
VMEM = pltpu.VMEM


def rotate(vectors, positions):
    half_dim = vectors.shape[-1] // 2
    freq_index = jnp.arange(half_dim, dtype=jnp.float32)
    inverse = jnp.power(jnp.float32(THETA), -2.0 * freq_index / vectors.shape[-1])
    angles = positions.astype(jnp.float32)[:, None] * inverse[None, :]
    cosine = jnp.cos(angles)[:, None, :]
    sine = jnp.sin(angles)[:, None, :]
    first = vectors[..., :half_dim]
    second = vectors[..., half_dim:]
    return jnp.concatenate(
        [first * cosine - second * sine, second * cosine + first * sine], axis=-1
    )


def bit_orders(levels):
    down = list(range(levels - 1, -1, -1))
    swapped = down[:-2] + [down[-1], down[-2]]
    low_first = [0, 1] + list(range(levels - 1, 1, -1))
    return [down, swapped, low_first]


def head_groups(heads):
    first = (heads + 2) // 3
    second = (heads - first + 1) // 2
    sizes = [first, second, heads - first - second]
    starts = [0, first, first + second]
    return list(zip(starts, sizes))


def span(bits):
    masks = [0]
    for bit in bits:
        masks = masks + [mask | (1 << bit) for mask in masks]
    return masks


def flipped(me, mask):
    out = me
    bit = 0
    while (1 << bit) <= mask:
        if mask & (1 << bit):
            out = out + (1 - 2 * (lax.rem(me // (1 << bit), 2))) * (1 << bit)
        bit += 1
    return out


def greet(levels, me, others=()):
    barrier = pltpu.get_barrier_semaphore()
    for other in others:
        pl.semaphore_signal(barrier, inc=1, device_id={"tp": other}, device_id_type=MESH)
    for bit in range(levels):
        pl.semaphore_signal(
            barrier, inc=1, device_id={"dp": flipped(me, 1 << bit)}, device_id_type=MESH
        )
    pl.semaphore_wait(barrier, levels + len(others))


def gather_kernel(levels, q_ref, out_ref, send_sem, recv_sem, own_sem):
    me = lax.axis_index("dp")
    greet(levels, me)
    groups = head_groups(q_ref.shape[0])
    orders = bit_orders(levels)
    sends = []
    own = pltpu.make_async_copy(q_ref, out_ref.at[me], own_sem)
    own.start()

    def copy_of(piece, mask, bit):
        start, size = groups[piece]
        block = flipped(me, mask)
        heads = pl.ds(start, size)
        key = mask | (1 << bit)
        source = q_ref.at[heads] if mask == 0 else out_ref.at[block, heads]
        return pltpu.make_async_remote_copy(
            src_ref=source,
            dst_ref=out_ref.at[block, heads],
            send_sem=send_sem.at[piece, key],
            recv_sem=recv_sem.at[piece, key],
            device_id={"dp": flipped(me, 1 << bit)},
            device_id_type=MESH,
        )

    def wait_arrival(piece, mask):
        start, size = groups[piece]
        landed = out_ref.at[flipped(me, mask), pl.ds(start, size)]
        pltpu.make_async_copy(landed, landed, recv_sem.at[piece, mask]).wait()

    for level in range(levels):
        for index in range(1 << level):
            for piece in range(3):
                if groups[piece][1] == 0:
                    continue
                order = orders[piece]
                mask = span(order[:level])[index]
                if mask and index >= (1 << (level - 1)):
                    wait_arrival(piece, mask)
                copy = copy_of(piece, mask, order[level])
                copy.start()
                sends.append(copy)
    for piece in range(3):
        if groups[piece][1]:
            for mask in span(orders[piece])[1 << (levels - 1) :]:
                wait_arrival(piece, mask)
    for copy in sends:
        copy.wait_send()
    own.wait()


def attend_kernel(
    per_owner, slot_ref, valid_ref, q_ref, kv_ref, nk_ref, nv_ref, part_ref, stat_ref
):
    me = lax.axis_index("dp")
    total, heads, rows, width = q_ref.shape
    kv_heads = kv_ref.shape[2]
    page = kv_ref.shape[3]
    shared = heads // kv_heads
    scale = 1.0 / math.sqrt(width)
    stat_row = lax.broadcasted_iota(jnp.int32, (8, rows), 0)

    def scores_of(keys, group, kv_head):
        queries = q_ref[group, kv_head * shared : (kv_head + 1) * shared]
        queries = queries.reshape(shared * rows, width)
        return (
            lax.dot_general(
                keys, queries, (((1,), (1,)), ((), ())), preferred_element_type=jnp.float32
            )
            * scale
        )

    def summed(scores, values):
        highest = jnp.max(scores, axis=0, keepdims=True)
        expo = jnp.exp(scores - highest)
        total_of = jnp.sum(expo, axis=0, keepdims=True)
        part = lax.dot_general(
            values,
            expo.astype(jnp.bfloat16),
            (((0,), (0,)), ((), ())),
            preferred_element_type=jnp.float32,
        )
        return highest, total_of, part

    def stats(highest, total_of):
        return jnp.where(stat_row < 4, highest, total_of)

    def one_group(group, carry):
        held = valid_ref[group, 0] > 0

        @pl.when(held)
        def _():
            row = lax.broadcasted_iota(jnp.int32, (page, 1), 0)
            ok = jnp.concatenate(
                [row < valid_ref[group, k] for k in range(per_owner)], axis=0
            )
            for kv_head in range(kv_heads):
                keys = jnp.concatenate(
                    [kv_ref[slot_ref[group, k], 0, kv_head] for k in range(per_owner)], axis=0
                )
                values = jnp.concatenate(
                    [kv_ref[slot_ref[group, k], 1, kv_head] for k in range(per_owner)], axis=0
                )
                scores = jnp.where(ok, scores_of(keys, group, kv_head), NEG)
                highest, total_of, part = summed(scores, values)
                for j in range(shared):
                    lanes = slice(j * rows, (j + 1) * rows)
                    part_ref[group, kv_head * shared + j] = part[:, lanes].astype(jnp.bfloat16)
                    stat_ref[group, kv_head * shared + j] = stats(
                        highest[:, lanes], total_of[:, lanes]
                    )

        @pl.when(jnp.logical_not(held))
        def _():
            for head in range(heads):
                part_ref[group, head] = jnp.zeros((width, rows), jnp.bfloat16)
                stat_ref[group, head] = jnp.where(stat_row < 4, NEG, 0.0)

        return carry

    lax.fori_loop(0, total, one_group, 0)

    key_row = lax.broadcasted_iota(jnp.int32, (rows, shared * rows), 0)
    token = lax.rem(lax.broadcasted_iota(jnp.int32, (rows, shared * rows), 1), rows)
    for kv_head in range(kv_heads):
        scores = jnp.where(key_row <= token, scores_of(nk_ref[kv_head], me, kv_head), NEG)
        highest, total_of, part = summed(scores, nv_ref[kv_head])
        for j in range(shared):
            head = kv_head * shared + j
            lanes = slice(j * rows, (j + 1) * rows)
            before = stat_ref[me, head]
            top, count, summed_part = merge(
                before[0:1],
                before[4:5],
                part_ref[me, head].astype(jnp.float32),
                highest[:, lanes],
                total_of[:, lanes],
                part[:, lanes],
            )
            part_ref[me, head] = summed_part.astype(jnp.bfloat16)
            stat_ref[me, head] = stats(top, count)


def merge(top_a, count_a, part_a, top_b, count_b, part_b):
    top = jnp.maximum(top_a, top_b)
    factor_a = jnp.exp(top_a - top)
    factor_b = jnp.exp(top_b - top)
    return (
        top,
        count_a * factor_a + count_b * factor_b,
        part_a * factor_a + part_b * factor_b,
    )


def home_kernel(levels, part_ref, stat_ref, out_ref, part_box, stat_box, part_send, part_recv, stat_send, stat_recv):
    me = lax.axis_index("dp")
    heads, width, rows = part_ref.shape[1:]
    groups = head_groups(heads)
    orders = [order[::-1] for order in bit_orders(levels)]
    stat_row = lax.broadcasted_iota(jnp.int32, (8, rows), 0)
    sends = []
    where = {}

    def held(piece, mask):
        if (piece, mask) in where:
            key = where[piece, mask]
            return part_box.at[key], stat_box.at[key]
        block = flipped(me, mask)
        return part_ref.at[block], stat_ref.at[block]

    def send(piece, level, mask):
        order = orders[piece]
        bit = 1 << order[level]
        cut = pl.ds(*groups[piece])
        part, stat = held(piece, mask)
        for source, box, out_sem, in_sem in (
            (part, part_box, part_send, part_recv),
            (stat, stat_box, stat_send, stat_recv),
        ):
            copy = pltpu.make_async_remote_copy(
                src_ref=source.at[cut],
                dst_ref=box.at[mask, cut],
                send_sem=out_sem.at[piece, mask],
                recv_sem=in_sem.at[piece, mask],
                device_id={"dp": flipped(me, bit)},
                device_id_type=MESH,
            )
            copy.start()
            sends.append(copy)

    def take(piece, level, mask):
        order = orders[piece]
        key = mask | (1 << order[level])
        start, size = groups[piece]
        cut = pl.ds(start, size)
        part, stat = held(piece, mask)
        for box, in_sem in ((part_box, part_recv), (stat_box, stat_recv)):
            landed = box.at[key, cut]
            pltpu.make_async_copy(landed, landed, in_sem.at[piece, key]).wait()
        last = level == levels - 1

        def one_head(head):
            mine = stat[head]
            came = stat_box[key, head]
            top, count, merged = merge(
                mine[0:1],
                mine[4:5],
                part[head].astype(jnp.float32),
                came[0:1],
                came[4:5],
                part_box[key, head].astype(jnp.float32),
            )
            return top, count, merged

        if last:
            for head in range(start, start + size):
                _, count, merged = one_head(head)
                out_ref[:, head * width : (head + 1) * width] = (merged / count).T.astype(
                    out_ref.dtype
                )
        else:

            def body(head, carry):
                top, count, merged = one_head(head)
                part_box[key, head] = merged.astype(jnp.bfloat16)
                stat_box[key, head] = jnp.where(stat_row < 4, top, count)
                return carry

            lax.fori_loop(start, start + size, body, 0)
            where[piece, mask] = key

    live = [piece for piece in range(3) if groups[piece][1]]
    for index in range(1 << (levels - 1)):
        for piece in live:
            order = orders[piece]
            send(piece, 0, span(order[:0:-1])[index] | (1 << order[0]))
    for level in range(levels):
        if level == levels - 1:
            for piece in live:
                take(piece, level, 0)
            break
        for forward in (True, False):
            for index in range(1 << (levels - 2 - level)):
                for piece in live:
                    order = orders[piece]
                    mask = span(order[: level + 1 : -1])[index]
                    if forward:
                        mask = mask | (1 << order[level + 1])
                    take(piece, level, mask)
                    if forward:
                        send(piece, level + 1, mask)
    for copy in sends:
        copy.wait_send()


def tail_kernel(
    levels,
    ranks,
    part_ref,
    stat_ref,
    tokens_ref,
    gain_ref,
    w_out_ref,
    w_gate_ref,
    w_up_ref,
    w_down_ref,
    context_ref,
    layer_ref,
    part_box,
    stat_box,
    part_send,
    part_recv,
    stat_send,
    stat_recv,
    out_buf,
    gate_buf,
    down_buf,
    attn_part,
    attn_box,
    stream_all,
    mlp_in,
    hidden,
    mlp_part,
    mlp_box,
    out_sem,
    gate_sem,
    down_sem,
    attn_send,
    attn_recv,
    stream_send,
    stream_recv,
    mlp_send,
    mlp_recv,
):
    rank = lax.axis_index("tp")
    share = tokens_ref.shape[1]
    model = mlp_in.shape[1]
    gate_slots, _, _, gate_width = gate_buf.shape
    down_slots, units, down_width = down_buf.shape
    gate_steps = units // gate_width
    per_target = share // down_width
    down_steps = ranks * per_target
    targets = [lax.rem(rank + 1 + t, ranks) for t in range(ranks)]

    def load_out(t):
        columns = pl.ds(pl.multiple_of(targets[t] * share, share), share)
        return pltpu.make_async_copy(w_out_ref.at[:, columns], out_buf.at[t], out_sem.at[t])

    def load_gate(step, which):
        slot = lax.rem(step, gate_slots)
        columns = pl.ds(pl.multiple_of(step * gate_width, gate_width), gate_width)
        source = (w_gate_ref, w_up_ref)[which]
        return pltpu.make_async_copy(
            source.at[:, columns], gate_buf.at[slot, which], gate_sem.at[slot, which]
        )

    def load_down(step):
        slot = lax.rem(step, down_slots)
        target = lax.rem(rank + 1 + step // per_target, ranks)
        start = target * share + lax.rem(step, per_target) * down_width
        columns = pl.ds(pl.multiple_of(start, down_width), down_width)
        return pltpu.make_async_copy(
            w_down_ref.at[:, columns], down_buf.at[slot], down_sem.at[slot]
        )

    for t in range(ranks):
        load_out(t).start()
    for step in range(min(gate_slots, gate_steps)):
        load_gate(step, 0).start()
        load_gate(step, 1).start()
    for step in range(min(down_slots, down_steps)):
        load_down(step).start()

    greet(levels, lax.axis_index("dp"), targets[:-1])
    home_kernel(
        levels,
        part_ref,
        stat_ref,
        context_ref,
        part_box,
        stat_box,
        part_send,
        part_recv,
        stat_send,
        stat_recv,
    )

    def to_target(source, box, t, send_sem, recv_sem):
        return pltpu.make_async_remote_copy(
            src_ref=source,
            dst_ref=box,
            send_sem=send_sem.at[t],
            recv_sem=recv_sem.at[t],
            device_id={"tp": targets[t]},
            device_id_type=MESH,
        )

    sends = []
    for t in range(ranks):
        load_out(t).wait()

        def project(step, carry, t=t):
            columns = pl.ds(pl.multiple_of(step * down_width, down_width), down_width)
            attn_part[t, :, columns] = jnp.dot(
                context_ref[...], out_buf[t, :, columns], preferred_element_type=jnp.float32
            ).astype(jnp.bfloat16)
            return carry

        lax.fori_loop(0, per_target, project, 0)
        if t < ranks - 1:
            copy = to_target(attn_part.at[t], attn_box.at[t], t, attn_send, attn_recv)
            copy.start()
            sends.append(copy)
    attn_sum = attn_part[ranks - 1].astype(jnp.float32)
    for t in range(ranks - 1):
        pltpu.make_async_copy(attn_box.at[t], attn_box.at[t], attn_recv.at[t]).wait()
        attn_sum = attn_sum + attn_box[t].astype(jnp.float32)
    stream_all[rank] = (tokens_ref[...].astype(jnp.float32) + attn_sum).astype(jnp.bfloat16)
    for t in range(ranks - 1):
        copy = to_target(stream_all.at[rank], stream_all.at[rank], t, stream_send, stream_recv)
        copy.start()
        sends.append(copy)
    for t in range(ranks - 1):
        landed = stream_all.at[lax.rem(rank + 2 * ranks - 1 - t, ranks)]
        pltpu.make_async_copy(landed, landed, stream_recv.at[t]).wait()
    squares = jnp.zeros((stream_all.shape[1], 1), jnp.float32)
    for block in range(ranks):
        piece = stream_all[block].astype(jnp.float32)
        squares = squares + jnp.sum(piece * piece, axis=-1, keepdims=True)
    factor = lax.rsqrt(squares / model + EPS)
    for block in range(ranks):
        lanes = slice(block * share, (block + 1) * share)
        piece = stream_all[block].astype(jnp.float32)
        mlp_in[:, lanes] = (piece * factor * gain_ref[:, lanes]).astype(jnp.bfloat16)

    def gate_step(step, carry):
        slot = lax.rem(step, gate_slots)
        load_gate(step, 0).wait()
        gate = jnp.dot(mlp_in[...], gate_buf[slot, 0], preferred_element_type=jnp.float32)
        load_gate(step, 1).wait()
        up = jnp.dot(mlp_in[...], gate_buf[slot, 1], preferred_element_type=jnp.float32)
        columns = pl.ds(pl.multiple_of(step * gate_width, gate_width), gate_width)
        hidden[:, columns] = (gate / (1.0 + jnp.exp(-gate)) * up).astype(jnp.bfloat16)

        @pl.when(step + gate_slots < gate_steps)
        def _():
            load_gate(step + gate_slots, 0).start()
            load_gate(step + gate_slots, 1).start()

        return carry

    lax.fori_loop(0, gate_steps, gate_step, 0)

    for t in range(ranks):

        def down_step(index, carry, t=t):
            step = index + t * per_target
            slot = lax.rem(step, down_slots)
            load_down(step).wait()
            columns = pl.ds(pl.multiple_of(index * down_width, down_width), down_width)
            mlp_part[t, :, columns] = jnp.dot(
                hidden[...], down_buf[slot], preferred_element_type=jnp.float32
            ).astype(jnp.bfloat16)

            @pl.when(step + down_slots < down_steps)
            def _():
                load_down(step + down_slots).start()

            return carry

        lax.fori_loop(0, per_target, down_step, 0)
        if t < ranks - 1:
            copy = to_target(mlp_part.at[t], mlp_box.at[t], t, mlp_send, mlp_recv)
            copy.start()
            sends.append(copy)
    mlp_sum = mlp_part[ranks - 1].astype(jnp.float32)
    for t in range(ranks - 1):
        pltpu.make_async_copy(mlp_box.at[t], mlp_box.at[t], mlp_recv.at[t]).wait()
        mlp_sum = mlp_sum + mlp_box[t].astype(jnp.float32)
    layer_ref[...] = (stream_all[rank].astype(jnp.float32) + mlp_sum).astype(jnp.bfloat16)
    for copy in sends:
        copy.wait_send()


def attention(
    queries, new_keys, new_values, kv_pool, slot_pick, valid, groups, per_owner, ranks, tail_args
):
    heads, rows, width = queries.shape
    levels = groups.bit_length() - 1
    vmem = pl.BlockSpec(memory_space=VMEM)
    smem = pl.BlockSpec(memory_space=pltpu.SMEM)
    dma = pltpu.SemaphoreType.DMA
    all_queries = pl.pallas_call(
        functools.partial(gather_kernel, levels),
        out_shape=jax.ShapeDtypeStruct((groups, heads, rows, width), jnp.bfloat16),
        in_specs=[vmem],
        out_specs=vmem,
        scratch_shapes=[dma((3, groups)), dma((3, groups)), dma],
        compiler_params=pltpu.CompilerParams(collective_id=0, has_side_effects=True),
        name="query_gather",
    )(queries)
    parts, stats = pl.pallas_call(
        functools.partial(attend_kernel, per_owner),
        out_shape=(
            jax.ShapeDtypeStruct((groups, heads, width, rows), jnp.bfloat16),
            jax.ShapeDtypeStruct((groups, heads, 8, rows), jnp.float32),
        ),
        in_specs=[smem, smem, vmem, vmem, vmem, vmem],
        out_specs=(vmem, vmem),
        name="page_attend",
    )(slot_pick, valid, all_queries, kv_pool, new_keys, new_values)
    tokens, gain, w_out, w_gate, w_up, w_down = tail_args
    share = tokens.shape[1]
    model, units = w_gate.shape
    gate_width = math.gcd(units, 256)
    down_width = math.gcd(share, 512)
    gate_slots, down_slots = 4, 3
    hbm = pl.BlockSpec(memory_space=pl.ANY)
    half = (ranks, rows, share)
    return pl.pallas_call(
        functools.partial(tail_kernel, levels, ranks),
        out_shape=(
            jax.ShapeDtypeStruct((rows, heads * width), jnp.bfloat16),
            jax.ShapeDtypeStruct((rows, share), jnp.bfloat16),
        ),
        in_specs=[vmem, vmem, vmem, vmem, hbm, hbm, hbm, hbm],
        out_specs=(vmem, vmem),
        scratch_shapes=[
            VMEM((groups, heads, width, rows), jnp.bfloat16),
            VMEM((groups, heads, 8, rows), jnp.float32),
            dma((3, groups)),
            dma((3, groups)),
            dma((3, groups)),
            dma((3, groups)),
            VMEM((ranks, heads * width, share), jnp.bfloat16),
            VMEM((gate_slots, 2, model, gate_width), jnp.bfloat16),
            VMEM((down_slots, units, down_width), jnp.bfloat16),
            VMEM(half, jnp.bfloat16),
            VMEM(half, jnp.bfloat16),
            VMEM(half, jnp.bfloat16),
            VMEM((rows, model), jnp.bfloat16),
            VMEM((rows, units), jnp.bfloat16),
            VMEM(half, jnp.bfloat16),
            VMEM(half, jnp.bfloat16),
            dma((ranks,)),
            dma((gate_slots, 2)),
            dma((down_slots,)),
            dma((ranks,)),
            dma((ranks,)),
            dma((ranks,)),
            dma((ranks,)),
            dma((ranks,)),
            dma((ranks,)),
        ],
        compiler_params=pltpu.CompilerParams(
            collective_id=1, has_side_effects=True, vmem_limit_bytes=66_000_000
        ),
        name="home_and_mlp",
    )(parts, stats, tokens, gain[None, :], w_out, w_gate, w_up, w_down)


def shards(
    tokens,
    norm_gain,
    w_query,
    w_key,
    w_value,
    w_out,
    mlp_gain,
    w_gate,
    w_up,
    w_down,
    kv_pool,
    prefix_len,
    page_owner,
    page_slot,
    serving,
):
    groups = lax.axis_size("dp")
    device = lax.axis_index("dp")
    new_tokens = tokens.shape[0]
    pages_max = page_owner.shape[1]
    per_owner = (pages_max + groups - 1) // groups
    page_len = kv_pool.shape[3]
    head_dim = kv_pool.shape[4]
    kv_heads = kv_pool.shape[2]
    q_heads = w_query.shape[1] // head_dim
    group_ids = jnp.arange(groups, dtype=jnp.int32)
    request = jnp.sum(jnp.where(group_ids == device, serving, 0))
    length = jnp.sum(jnp.where(group_ids == request, prefix_len, 0))
    gathered = lax.all_gather(tokens, "tp", axis=1, tiled=True)
    gathered_f32 = gathered.astype(jnp.float32)
    in_scale = lax.rsqrt(jnp.mean(gathered_f32 * gathered_f32, axis=-1, keepdims=True) + EPS)
    normed = (gathered_f32 * in_scale * norm_gain).astype(jnp.bfloat16)
    positions = length + jnp.arange(new_tokens, dtype=jnp.int32)
    queries = rotate(
        jnp.dot(normed, w_query, preferred_element_type=jnp.float32).reshape(
            new_tokens, q_heads, head_dim
        ),
        positions,
    ).astype(jnp.bfloat16)
    new_keys = rotate(
        jnp.dot(normed, w_key, preferred_element_type=jnp.float32).reshape(
            new_tokens, kv_heads, head_dim
        ),
        positions,
    ).astype(jnp.bfloat16)
    new_values = (
        jnp.dot(normed, w_value, preferred_element_type=jnp.float32)
        .astype(jnp.bfloat16)
        .reshape(new_tokens, kv_heads, head_dim)
    )
    owner_dest = jnp.take(page_owner, serving, axis=0)
    slot_dest = jnp.take(page_slot, serving, axis=0)
    length_dest = jnp.take(prefix_len, serving)
    page_ids = jnp.arange(pages_max, dtype=jnp.int32)
    owned = owner_dest == device
    rank = jnp.cumsum(owned.astype(jnp.int32), axis=1) - 1
    valid_dest = jnp.clip(length_dest[:, None] - page_ids[None, :] * page_len, 0, page_len)
    choose = jnp.arange(per_owner, dtype=jnp.int32)
    picked = owned[:, None, :] & (rank[:, None, :] == choose[None, :, None])
    slot_pick = jnp.sum(jnp.where(picked, slot_dest[:, None, :], 0), axis=2)
    valid = jnp.sum(jnp.where(picked, valid_dest[:, None, :], 0), axis=2)
    return attention(
        queries.transpose(1, 0, 2),
        new_keys.transpose(1, 0, 2),
        new_values.transpose(1, 0, 2),
        kv_pool,
        slot_pick,
        valid,
        groups,
        per_owner,
        lax.axis_size("tp"),
        (tokens, mlp_gain, w_out, w_gate, w_up, w_down),
    )


def solution(mesh):
    in_specs = (
        P("dp", "tp"),
        P(),
        P(None, "tp"),
        P(None, "tp"),
        P(None, "tp"),
        P("tp", None),
        P(),
        P(None, "tp"),
        P(None, "tp"),
        P("tp", None),
        P("dp", None, "tp", None, None),
        P(),
        P(),
        P(),
        P(),
    )
    out_specs = (P("dp", "tp"), P("dp", "tp"))
    return jax.shard_map(shards, mesh=mesh, in_specs=in_specs, out_specs=out_specs, check_vma=False)
```

profile of v0, /device:TPU:1, one launch (start us, length us, event | category | flops | bytes accessed | tf_op | source)
XLA Modules:
  0.0 198.9 jit_solution(10980445953078624731)
XLA Ops:
  7.2 0.7 all-gather.2.cloned.1.call-update
  7.9 0.7 compare_select_fusion
  8.6 1.3 gather_fusion
  9.9 0.6 gather_fusion.1
  10.5 1.3 broadcast_select_fusion.1
  12.1 1.3 gather_fusion.2
  13.7 0.7 copy.34.valid_ref
  14.4 0.7 copy.33.slot_ref
  15.0 1.9 fusion.5
  17.0 0.7 add_convert_fusion.2
  17.6 0.3 multiply_cosine_fusion
  18.0 3.1 %all-gather.2.cloned.1.call-done = bf16[128,4096]{1,0:T(8,128)(2,1)} async-done(((bf16[128,2048]{1,0:T(8,128)(2,1)}), bf16[128,4096]{1,0:T(8,128)(2,1)}) %all-gather.2.cloned.1.call-update) | async-done | bytes 1048592 | tf_op jit(solution)/shard_map/all_gather | solution.py:624
  21.1 1.5 fusion
  22.6 1.8 convolution_convert_fusion
  24.6 0.8 copy.32
  25.3 2.6 %fusion.7 = f32[128,256]{0,1:T(8,128)S(1)} fusion(bf16[4096,256]{1,0:T(8,128)(2,1)} %param.20, bf16[128,4096]{1,0:T(8,128)(2,1)S(1)} %copy-done.2, f32[4096]{0:T(1024)S(1)} %copy-done.3, f32[128]{0:T(128)S(1)} %add_rsqrt_fusion), kind=kOutput, calls=%fused_computation.37 | convolution fusion | flops 270532608 | bytes 3293696 | tf_op jit(solution)/shard_map/dot_general | solution.py:636
  28.0 6.8 %fusion.9 = f32[128,1024]{0,1:T(8,128)S(1)} fusion(bf16[4096,1024]{1,0:T(8,128)(2,1)} %param.19, bf16[128,4096]{1,0:T(8,128)(2,1)S(1)} %copy-done.2, f32[4096]{0:T(1024)S(1)} %copy-done.3, f32[128]{0:T(128)S(1)} %add_rsqrt_fusion), kind=kOutput, calls=%fused_computation.38 | convolution fusion | flops 1075838976 | bytes 9978368 | tf_op jit(solution)/shard_map/dot_general | solution.py:630
  35.6 0.9 maximum_bitcast_fusion.q_ref
  36.5 46.4 %query_gather.1.q_ref = bf16[16,8,128,128]{3,2,1,0:T(8,128)(2,1)} custom-call(bf16[8,128,128]{2,1,0:T(8,128)(2,1)} %maximum_bitcast_fusion.q_ref), custom_call_target="tpu_custom_call" | custom-call | tf_op jit(solution)/shard_map/query_gather/pallas_call | solution.py:526
  82.9 0.7 maximum_bitcast_fusion.1.nk_ref
  83.6 21.5 %page_attend.1 = (bf16[16,8,128,128]{3,2,1,0:T(8,128)(2,1)}, f32[16,8,8,128]{3,2,1,0:T(8,128)}) custom-call(s32[16,4]{1,0:T(8,128)} %copy.33.slot_ref, s32[16,4]{1,0:T(8,128)} %copy.34.valid_ref, bf16[16,8,128,128]{3,2,1,0:T(8,128)(2,1)} %query_gather.1.q_ref, bf16[64,2,2,128,128]{4,3,2,1,0:T(8,128)(2,1)} %kv_ref.1, ...), custom_call_target="tpu_custom_call" | custom-call | tf_op jit(solution)/shard_map/page_attend/pallas_call | solution.py:535
  105.1 83.4 %home_and_mlp.1 = (bf16[128,1024]{1,0:T(8,128)(2,1)}, bf16[128,2048]{1,0:T(8,128)(2,1)}) custom-call(bf16[16,8,128,128]{3,2,1,0:T(8,128)(2,1)} %get-tuple-element.5.part_ref, f32[16,8,8,128]{3,2,1,0:T(8,128)} %get-tuple-element.6.stat_ref, bf16[128,2048]{1,0:T(8,128)(2,1)} %tokens_ref.1, f32[1,4096]{1,0:T(1,128)} %bitcast.16, bf16[1024,4096]{1,0:T(8,128)(2,1)} %w_out_ref.1, ...), custom_call_target="tpu_custom_call" | custom-call | tf_op jit(solution)/shard_map/home_and_mlp/pallas_call | solution.py:553
  188.5 1.7 copy.43
  190.2 1.9 copy.44
  (29 shorter events, 1.6 us)
Async XLA Ops:
  7.2 2.8 %copy-start = (s32[16,64]{1,0:T(8,128)S(1)}, s32[16,64]{1,0:T(8,128)}, u32[]{:S(2)}) copy-start(s32[16,64]{1,0:T(8,128)} %param.29) | copy-start | bytes 12292
  7.2 15.4 %copy-start.3 = (f32[4096]{0:T(1024)S(1)}, f32[4096]{0:T(1024)}, u32[]{:S(2)}) copy-start(f32[4096]{0:T(1024)} %param.18) | copy-start | bytes 49156
  7.2 15.4 %copy-start.4 = (bf16[4096,256]{1,0:T(8,128)(2,1)S(1)}, bf16[4096,256]{1,0:T(8,128)(2,1)}, u32[]{:S(2)}) copy-start(bf16[4096,256]{1,0:T(8,128)(2,1)} %param.21) | copy-start | bytes 6291460
  7.2 13.9 %all-gather.2.cloned.1.call-start = ((), (), s32[]{:S(2)}) async-start(), calls=%async_computation | async-start | bytes 1572864 | tf_op jit(solution)/shard_map/all_gather | solution.py:624
  22.6 2.8 %copy-start.2 = (bf16[128,4096]{1,0:T(8,128)(2,1)S(1)}, bf16[128,4096]{1,0:T(8,128)(2,1)}, u32[]{:S(2)}) copy-start(bf16[128,4096]{1,0:T(8,128)(2,1)} %all-gather.2.cloned.1.call-done) | copy-start | bytes 3145732
  105.1 86.9 %copy-start.1 = (s32[16,64]{1,0:T(8,128)S(1)}, s32[16,64]{1,0:T(8,128)}, u32[]{:S(2)}) copy-start(s32[16,64]{1,0:T(8,128)} %param.29) | copy-start | bytes 12292
Sparse Core Ops, SparseCore 0:
  9.6 11.4 all-gather.1
where the time goes:
time: 200 us; the launch traced here: 199 us
  Pallas kernels  151 us (76%)
  between operations  14.2 us (7%)
  matrix products  11.3 us (6%)
  local copies, waits for them, and re-layouts  9.59 us (5%)
  other arithmetic  8.76 us (4%)
  waiting for transfers between devices  3.79 us (2%)
    pallas_call x1, Pallas kernels, attention(): pl.pallas_call(functools.partial(tail_kernel, levels, ranks), out_shape=(...  83.4 us
    pallas_call x1, Pallas kernels, attention(): pl.pallas_call(functools.partial(gather_kernel, levels), out_shape=jax.Sh...  46.4 us
    pallas_call x1, Pallas kernels, attention(): pl.pallas_call(functools.partial(attend_kernel, per_owner), out_shape=(ja...  21.5 us
    dot_general x1, matrix products, shards(): jnp.dot(normed, w_query, preferred_element_type=jnp.float32)  6.82 us
    unnamed x16, local copies, waits for them, and re-layouts  4.17 us
  transfers between devices with their start and end apart: 1, of which 1 were waited for; matrix products, arithmetic and copies ran while one was open for 5% of the time, Pallas kernels for 0%

commit v1 on v0

v1 whole, which is shorter than its diff:
```python
import functools
import math

import jax
import jax.numpy as jnp
from jax import lax
from jax.experimental import pallas as pl
from jax.experimental.pallas import tpu as pltpu
from jax.sharding import PartitionSpec as P

EPS = 1e-05
THETA = 500000.0
NEG = -1e30
LOG2E = 1.4426950408889634
MESH = pl.DeviceIdType.MESH
VMEM = pltpu.VMEM
VMEM_BUDGET = 66_800_000
TILE = 256


def xor(a, b, bits):
    out = 0
    for bit in range(bits):
        unit = 1 << bit
        out = out + lax.rem(lax.div(a, unit) + lax.div(b, unit), 2) * unit
    return out


def merge_stats(left, right):
    shared = left.shape[0] // 2
    top = jnp.maximum(left[:shared], right[:shared])
    factor_left = jnp.exp2(left[:shared] - top)
    factor_right = jnp.exp2(right[:shared] - top)
    count = left[shared:] * factor_left + right[shared:] * factor_right
    return jnp.concatenate([top, count], axis=0), factor_left, factor_right


def layer_kernel(
    plan,
    slot_ref,
    valid_ref,
    cos_ref,
    sin_ref,
    gain_ref,
    mlp_gain_ref,
    tokens_ref,
    wq_ref,
    wk_ref,
    wv_ref,
    wo_ref,
    wg_ref,
    wu_ref,
    wd_ref,
    kv_ref,
    context_ref,
    layer_ref,
    ring,
    kv_buf,
    tok_all,
    normed,
    q_all,
    new_k,
    new_v,
    part,
    stat,
    box,
    stat_box,
    attn_all,
    hidden,
    mlp_part,
    mlp_box,
    ring_sem,
    kv_sem,
    tok_sem,
    tok_send,
    tok_recv,
    q_send,
    q_recv,
    part_send,
    part_recv,
    stat_send,
    stat_recv,
    attn_send,
    attn_recv,
    mlp_send,
    mlp_recv,
):
    groups, ranks, kv_heads, per_owner = plan
    me = lax.axis_index("dp")
    rank = lax.axis_index("tp")
    bits = groups.bit_length() - 1
    planes = groups // 4
    rows, model = normed.shape
    share = tokens_ref.shape[1]
    width = q_all.shape[3]
    heads = q_all.shape[1]
    shared = heads // kv_heads
    page = kv_ref.shape[3]
    slots = ring.shape[0]
    units = wd_ref.shape[0]
    own_rows = wo_ref.shape[0]
    peers = [lax.rem(rank + 1 + t, ranks) for t in range(ranks - 1)]

    def slabs(total):
        step = math.gcd(total, TILE)
        return step, total // step

    q_width, q_tiles = slabs(wq_ref.shape[1])
    k_width, k_tiles = slabs(wk_ref.shape[1])
    g_width, g_tiles = slabs(units)
    d_width, d_tiles = slabs(share)
    d_tiles = d_tiles * ranks
    o_stack = model // own_rows
    o_cols = o_stack * TILE
    o_tiles = model // o_cols
    first_k = q_tiles
    first_v = first_k + k_tiles
    first_o = first_v + k_tiles
    first_g = first_o + o_tiles
    first_d = first_g + 2 * g_tiles
    last = first_d + d_tiles

    def slot_of(tile):
        return tile % slots if isinstance(tile, int) else lax.rem(tile, slots)

    def column_copy(source, start, step, tile):
        slot = slot_of(tile)
        count = source.shape[0]
        columns = pl.ds(pl.multiple_of(start, step), step)
        return pltpu.make_async_copy(
            source.at[:, columns],
            ring.at[slot, pl.ds(0, count), pl.ds(0, step)],
            ring_sem.at[slot],
        )

    def q_copy(i):
        return column_copy(wq_ref, i * q_width, q_width, i)

    def k_copy(i):
        return column_copy(wk_ref, i * k_width, k_width, first_k + i)

    def v_copy(i):
        return column_copy(wv_ref, i * k_width, k_width, first_v + i)

    def gate_copy(i, which):
        return column_copy((wg_ref, wu_ref)[which], i * g_width, g_width, first_g + 2 * i + which)

    def down_copy(i):
        per = d_tiles // ranks
        target = lax.rem(rank + 1 + i // per, ranks)
        return column_copy(wd_ref, target * share + (i % per) * d_width, d_width, first_d + i)

    def out_start(i):
        slot = slot_of(first_o + i)
        for s in range(o_stack):
            pltpu.make_async_copy(
                wo_ref.at[:, pl.ds(i * o_cols + s * TILE, TILE)],
                ring.at[slot, pl.ds(s * own_rows, own_rows), :],
                ring_sem.at[slot],
            ).start()

    def out_wait(i):
        slot = slot_of(first_o + i)
        pltpu.make_async_copy(ring.at[slot], ring.at[slot], ring_sem.at[slot]).wait()

    def start_tile(tile):
        if tile >= last:
            return
        if tile < first_k:
            q_copy(tile).start()
        elif tile < first_v:
            k_copy(tile - first_k).start()
        elif tile < first_o:
            v_copy(tile - first_v).start()
        elif tile < first_g:
            out_start(tile - first_o)
        elif tile < first_d:
            gate_copy((tile - first_g) // 2, (tile - first_g) % 2).start()
        else:
            down_copy(tile - first_d).start()

    own_columns = pl.ds(pl.multiple_of(rank * share, share), share)
    own_load = pltpu.make_async_copy(tokens_ref, tok_all.at[:, own_columns], tok_sem)
    own_load.start()
    for tile in range(first_o):
        start_tile(tile)

    x_to = me + 1 - 2 * lax.rem(me, 2)
    y_to = me + 2 - 4 * lax.rem(lax.div(me, 2), 2)
    hops = ((x_to, y_to), (y_to, x_to))

    barrier = pltpu.get_barrier_semaphore()
    for peer in peers:
        pl.semaphore_signal(barrier, inc=1, device_id={"tp": peer}, device_id_type=MESH)
    near = [x_to, y_to] + [xor(me, 4 * j, bits) for j in range(1, planes)]
    for other in near:
        pl.semaphore_signal(barrier, inc=1, device_id={"dp": other}, device_id_type=MESH)
    pl.semaphore_wait(barrier, len(near) + len(peers))

    def to_peer(source, target, send_sem, recv_sem, peer):
        return pltpu.make_async_remote_copy(
            src_ref=source,
            dst_ref=target,
            send_sem=send_sem,
            recv_sem=recv_sem,
            device_id={"tp": peer},
            device_id_type=MESH,
        )

    sends = []
    for t, peer in enumerate(peers):
        copy = to_peer(
            tokens_ref, tok_all.at[:, own_columns], tok_send.at[t], tok_recv.at[t], peer
        )
        copy.start()
        sends.append(copy)
    kv_load = pltpu.make_async_copy(kv_ref, kv_buf, kv_sem)
    kv_load.start()
    own_load.wait()
    for t in range(ranks - 1):
        came = lax.rem(rank + 2 * ranks - 1 - t, ranks)
        landed = tok_all.at[:, pl.ds(pl.multiple_of(came * share, share), share)]
        pltpu.make_async_copy(landed, landed, tok_recv.at[t]).wait()

    def normalize(gain):
        squares = jnp.zeros((rows, 1), jnp.float32)
        for start in range(0, model, share):
            piece = tok_all[:, start : start + share].astype(jnp.float32)
            squares = squares + jnp.sum(piece * piece, axis=-1, keepdims=True)
        factor = lax.rsqrt(squares / model + EPS)
        for start in range(0, model, share):
            piece = tok_all[:, start : start + share].astype(jnp.float32)
            normed[:, start : start + share] = (
                piece * factor * gain[:, start : start + share]
            ).astype(jnp.bfloat16)

    normalize(gain_ref)

    def rope(values):
        return values * cos_ref[...] + pltpu.roll(values, width // 2, 1) * sin_ref[...]

    def send_query(piece, block, target, key):
        cut = pl.ds(piece * shared, shared)
        pltpu.make_async_remote_copy(
            src_ref=q_all.at[block, cut],
            dst_ref=q_all.at[block, cut],
            send_sem=q_send.at[piece, key],
            recv_sem=q_recv.at[piece, key],
            device_id={"dp": target},
            device_id_type=MESH,
        ).start()

    def block_of(piece, key):
        if piece % 2:
            low = lax.rem(key, 4)
            key = key - low + lax.div(low, 2) + 2 * lax.rem(low, 2)
        return xor(me, key, bits)

    tiles_each = q_tiles // kv_heads
    per_tile = q_width // width
    for piece in range(kv_heads):

        def project(t, carry, piece=piece):
            tile = piece * tiles_each + t
            q_copy(tile).wait()
            values = jnp.dot(
                normed[...],
                ring[slot_of(tile), :, 0:q_width],
                preferred_element_type=jnp.float32,
            )
            for h in range(per_tile):
                q_all[me, tile * per_tile + h] = rope(
                    values[:, h * width : (h + 1) * width]
                ).astype(jnp.bfloat16)
            return carry

        lax.fori_loop(0, tiles_each, project, 0)
        for link in range(2):
            send_query(piece, me, hops[piece % 2][link], 1 + link)
        for j in range(1, planes):
            send_query(piece, me, xor(me, 4 * j, bits), 4 * j)

    for i in range(k_tiles):
        k_copy(i).wait()
        values = jnp.dot(
            normed[...], ring[first_k + i, :, 0:k_width], preferred_element_type=jnp.float32
        )
        for h in range(k_width // width):
            new_k[i * (k_width // width) + h] = rope(
                values[:, h * width : (h + 1) * width]
            ).astype(jnp.bfloat16)
    for i in range(k_tiles):
        v_copy(i).wait()
        values = jnp.dot(
            normed[...], ring[first_v + i, :, 0:k_width], preferred_element_type=jnp.float32
        )
        for h in range(k_width // width):
            new_v[i * (k_width // width) + h] = values[:, h * width : (h + 1) * width].astype(
                jnp.bfloat16
            )
    for tile in range(first_o, slots + first_o):
        start_tile(tile)
    kv_load.wait()

    scale = LOG2E / math.sqrt(width)

    def attend(keys, values, ok, block, piece):
        queries = q_all[block, piece * shared : (piece + 1) * shared]
        queries = queries.reshape(shared * rows, width)
        scores = lax.dot_general(
            keys, queries, (((1,), (1,)), ((), ())), preferred_element_type=jnp.float32
        )
        scores = jnp.where(ok, scores * scale, NEG)
        highest = jnp.max(scores, axis=0, keepdims=True)
        expo = jnp.exp2(scores - highest)
        count = jnp.sum(expo, axis=0, keepdims=True)
        summed = lax.dot_general(
            values,
            expo.astype(jnp.bfloat16),
            (((0,), (0,)), ((), ())),
            preferred_element_type=jnp.float32,
        )
        return highest, count, summed

    def keep(found, part_to, stat_to):
        highest, count, summed = found
        for j in range(shared):
            lanes = slice(j * rows, (j + 1) * rows)
            part_to[j] = summed[:, lanes].astype(jnp.bfloat16)
            stat_to[j : j + 1] = highest[:, lanes]
            stat_to[shared + j : shared + j + 1] = count[:, lanes]

    key_row = lax.broadcasted_iota(jnp.int32, (rows, shared * rows), 0)
    token = lax.rem(lax.broadcasted_iota(jnp.int32, (rows, shared * rows), 1), rows)
    for piece in range(kv_heads):
        keep(
            attend(new_k[piece], new_v[piece], key_row <= token, me, piece),
            box.at[piece, 0],
            stat_box.at[piece, 0],
        )

    def send_part(piece, block, target, key):
        for source, target_box, out_sem, in_sem in (
            (part, box, part_send, part_recv),
            (stat, stat_box, stat_send, stat_recv),
        ):
            pltpu.make_async_remote_copy(
                src_ref=source.at[block, piece],
                dst_ref=target_box.at[piece, key],
                send_sem=out_sem.at[piece, key],
                recv_sem=in_sem.at[piece, key],
                device_id={"dp": target},
                device_id_type=MESH,
            ).start()

    def landed_part(piece, key):
        for target_box, in_sem in ((box, part_recv), (stat_box, stat_recv)):
            landed = target_box.at[piece, key]
            pltpu.make_async_copy(landed, landed, in_sem.at[piece, key]).wait()

    def landed_query(piece, key, block):
        landed = q_all.at[block, pl.ds(piece * shared, shared)]
        pltpu.make_async_copy(landed, landed, q_recv.at[piece, key]).wait()

    row = lax.broadcasted_iota(jnp.int32, (page, 1), 0)

    def one_key(key, carry):
        turn = lax.rem(key, 4)
        for piece in range(kv_heads):
            block = block_of(piece, key)
            near_to, far_to = hops[piece % 2]

            @pl.when(key > 0)
            def _():
                landed_query(piece, key, block)

                @pl.when(turn == 0)
                def _():
                    send_query(piece, block, near_to, key + 1)

                @pl.when(turn < 2)
                def _():
                    send_query(piece, block, far_to, key + 2)

            pages = [slot_ref[block, k] for k in range(per_owner)]
            ok = jnp.concatenate([row < valid_ref[block, k] for k in range(per_owner)], axis=0)
            keys = jnp.concatenate([kv_buf[p, 0, piece] for p in pages], axis=0)
            values = jnp.concatenate([kv_buf[p, 1, piece] for p in pages], axis=0)
            keep(
                attend(keys, values, ok, block, piece),
                part.at[block, piece],
                stat.at[block, piece],
            )

            @pl.when(turn >= 2)
            def _():
                send_part(piece, block, far_to, key)

        return carry

    lax.fori_loop(0, groups, one_key, 0)

    def merge_into(piece, block, key):
        merged, mine, other = merge_stats(stat[block, piece], stat_box[piece, key])
        for j in range(shared):
            part[block, piece, j] = (
                part[block, piece, j].astype(jnp.float32) * mine[j : j + 1]
                + box[piece, key, j].astype(jnp.float32) * other[j : j + 1]
            ).astype(jnp.bfloat16)
        stat[block, piece] = merged

    def first_merges(index, carry):
        base = 4 * (planes - 1 - index)
        for turn in (1, 0):
            for piece in range(kv_heads):
                block = block_of(piece, base + turn)
                landed_part(piece, base + turn + 2)
                merge_into(piece, block, base + turn + 2)
                if turn:
                    send_part(piece, block, hops[piece % 2][0], base + 1)
        return carry

    lax.fori_loop(0, planes, first_merges, 0)

    def second_merges(index, carry):
        base = 4 * (planes - 1 - index)
        for piece in range(kv_heads):
            block = block_of(piece, base)
            landed_part(piece, base + 1)
            merge_into(piece, block, base + 1)

            @pl.when(base > 0)
            def _():
                send_part(piece, block, block, base)

        return carry

    lax.fori_loop(0, planes, second_merges, 0)

    for piece in range(kv_heads):

        def home_merge(j, carry, piece=piece):
            @pl.when(j > 0)
            def _():
                landed_part(piece, 4 * j)

            merged, mine, other = merge_stats(carry[0], stat_box[piece, 4 * j])
            sums = tuple(
                carry[1 + h] * mine[h : h + 1]
                + box[piece, 4 * j, h].astype(jnp.float32) * other[h : h + 1]
                for h in range(shared)
            )
            return (merged,) + sums

        start = (stat[me, piece],) + tuple(
            part[me, piece, h].astype(jnp.float32) for h in range(shared)
        )
        done = lax.fori_loop(0, planes, home_merge, start)
        for h in range(shared):
            lanes = slice((piece * shared + h) * width, (piece * shared + h + 1) * width)
            total = done[0][shared + h : shared + h + 1]
            context_ref[:, lanes] = (done[1 + h] / total).T.astype(jnp.bfloat16)

    for i in range(o_tiles):
        out_wait(i)
        for s in range(o_stack):
            start = i * o_cols + s * TILE
            attn_all[rank, :, start : start + TILE] = jnp.dot(
                context_ref[...],
                ring[slot_of(first_o + i), s * own_rows : (s + 1) * own_rows, :],
                preferred_element_type=jnp.float32,
            ).astype(jnp.bfloat16)
        start_tile(first_o + i + slots)
        for t, peer in enumerate(peers):
            ready = attn_all.at[rank, :, pl.ds(i * o_cols, o_cols)]
            copy = to_peer(ready, ready, attn_send.at[t, i], attn_recv.at[t, i], peer)
            copy.start()
            sends.append(copy)
    for i in range(o_tiles):
        columns = pl.ds(i * o_cols, o_cols)
        for t in range(ranks - 1):
            landed = attn_all.at[lax.rem(rank + 2 * ranks - 1 - t, ranks), :, columns]
            pltpu.make_async_copy(landed, landed, attn_recv.at[t, i]).wait()
        attn_sum = attn_all[0, :, columns].astype(jnp.float32)
        for r in range(1, ranks):
            attn_sum = attn_sum + attn_all[r, :, columns].astype(jnp.float32)
        tok_all[:, columns] = (tok_all[:, columns].astype(jnp.float32) + attn_sum).astype(
            jnp.bfloat16
        )

    normalize(mlp_gain_ref)

    def gate_step(i, carry):
        gate_copy(i, 0).wait()
        gate = jnp.dot(
            normed[...],
            ring[slot_of(first_g + 2 * i), :, 0:g_width],
            preferred_element_type=jnp.float32,
        )
        gate_copy(i, 1).wait()
        up = jnp.dot(
            normed[...],
            ring[slot_of(first_g + 2 * i + 1), :, 0:g_width],
            preferred_element_type=jnp.float32,
        )
        columns = pl.ds(pl.multiple_of(i * g_width, g_width), g_width)
        hidden[:, columns] = (gate / (1.0 + jnp.exp(-gate)) * up).astype(jnp.bfloat16)
        later = i + slots // 2

        @pl.when(later < g_tiles)
        def _():
            gate_copy(later, 0).start()
            gate_copy(later, 1).start()

        for which in range(2):
            down = 2 * (later - g_tiles) + which

            @pl.when((later >= g_tiles) & (down < d_tiles))
            def _():
                down_copy(down).start()

        return carry

    lax.fori_loop(0, g_tiles, gate_step, 0)

    per_target = d_tiles // ranks
    for t in range(ranks):

        def down_step(index, carry, t=t):
            i = index + t * per_target
            down_copy(i).wait()
            columns = pl.ds(pl.multiple_of(index * d_width, d_width), d_width)
            mlp_part[t, :, columns] = jnp.dot(
                hidden[...],
                ring[slot_of(first_d + i), 0:units, 0:d_width],
                preferred_element_type=jnp.float32,
            ).astype(jnp.bfloat16)

            @pl.when(i + slots < d_tiles)
            def _():
                down_copy(i + slots).start()

            return carry

        lax.fori_loop(0, per_target, down_step, 0)
        if t < ranks - 1:
            copy = to_peer(
                mlp_part.at[t], mlp_box.at[t], mlp_send.at[t], mlp_recv.at[t], peers[t]
            )
            copy.start()
            sends.append(copy)
    mlp_sum = mlp_part[ranks - 1].astype(jnp.float32)
    for t in range(ranks - 1):
        pltpu.make_async_copy(mlp_box.at[t], mlp_box.at[t], mlp_recv.at[t]).wait()
        mlp_sum = mlp_sum + mlp_box[t].astype(jnp.float32)
    layer_ref[...] = (tok_all[:, own_columns].astype(jnp.float32) + mlp_sum).astype(jnp.bfloat16)

    for copy in sends:
        copy.wait_send()

    def settle(key, carry):
        for piece in range(kv_heads):
            sent = q_all.at[0, pl.ds(piece * shared, shared)]
            pltpu.make_async_copy(sent, sent, q_send.at[piece, key]).wait()
            for source, out_sem in ((part, part_send), (stat, stat_send)):
                sent = source.at[0, piece]
                pltpu.make_async_copy(sent, sent, out_sem.at[piece, key]).wait()
        return carry

    lax.fori_loop(1, groups, settle, 0)


def layer(groups, ranks, per_owner, tables, gains, tokens, weights, kv_pool):
    slot_pick, valid, cosine, sine = tables
    rows, share = tokens.shape
    model = share * ranks
    _, _, kv_heads, page, width = kv_pool.shape
    heads = weights[0].shape[1] // width
    units = weights[4].shape[1]
    shared = heads // kv_heads
    bf16 = jnp.bfloat16
    dma = pltpu.SemaphoreType.DMA
    vmem = pl.BlockSpec(memory_space=VMEM)
    smem = pl.BlockSpec(memory_space=pltpu.SMEM)
    hbm = pl.BlockSpec(memory_space=pl.ANY)
    buffers = [
        (kv_pool.shape, bf16),
        ((rows, model), bf16),
        ((rows, model), bf16),
        ((groups, heads, rows, width), bf16),
        ((kv_heads, rows, width), bf16),
        ((kv_heads, rows, width), bf16),
        ((groups, kv_heads, shared, width, rows), bf16),
        ((groups, kv_heads, 2 * shared, rows), jnp.float32),
        ((kv_heads, groups, shared, width, rows), bf16),
        ((kv_heads, groups, 2 * shared, rows), jnp.float32),
        ((ranks, rows, model), bf16),
        ((rows, units), bf16),
        ((ranks, rows, share), bf16),
        ((ranks, rows, share), bf16),
    ]
    used = sum(math.prod(shape) * jnp.dtype(kind).itemsize for shape, kind in buffers)
    used += 2 * rows * (heads * width + share) + 8 * rows * width + 64 * model + 2_500_000
    slots = (VMEM_BUDGET - used) // (2 * model * TILE) // 2 * 2
    return pl.pallas_call(
        functools.partial(layer_kernel, (groups, ranks, kv_heads, per_owner)),
        out_shape=(
            jax.ShapeDtypeStruct((rows, heads * width), bf16),
            jax.ShapeDtypeStruct((rows, share), bf16),
        ),
        in_specs=[smem, smem, vmem, vmem, vmem, vmem] + [hbm] * 9,
        out_specs=(vmem, vmem),
        scratch_shapes=[VMEM((slots, model, TILE), bf16)]
        + [VMEM(shape, kind) for shape, kind in buffers]
        + [
            dma((slots,)),
            dma,
            dma,
            dma((ranks,)),
            dma((ranks,)),
            dma((kv_heads, groups)),
            dma((kv_heads, groups)),
            dma((kv_heads, groups)),
            dma((kv_heads, groups)),
            dma((kv_heads, groups)),
            dma((kv_heads, groups)),
            dma((ranks, 8)),
            dma((ranks, 8)),
            dma((ranks,)),
            dma((ranks,)),
        ],
        compiler_params=pltpu.CompilerParams(
            collective_id=0, has_side_effects=True, vmem_limit_bytes=67_000_000
        ),
        name="layer",
    )(slot_pick, valid, cosine, sine, *gains, tokens, *weights, kv_pool)


def shards(
    tokens,
    norm_gain,
    w_query,
    w_key,
    w_value,
    w_out,
    mlp_gain,
    w_gate,
    w_up,
    w_down,
    kv_pool,
    prefix_len,
    page_owner,
    page_slot,
    serving,
):
    groups = lax.axis_size("dp")
    device = lax.axis_index("dp")
    rows = tokens.shape[0]
    pages_max = page_owner.shape[1]
    per_owner = (pages_max + groups - 1) // groups
    page_len = kv_pool.shape[3]
    width = kv_pool.shape[4]
    ids = jnp.arange(groups, dtype=jnp.int32)
    served = serving[:, None] == ids[None, :]
    lengths = jnp.sum(jnp.where(served, prefix_len[None, :], 0), axis=1)
    length = jnp.sum(jnp.where(ids == device, lengths, 0))
    half = jnp.arange(width // 2, dtype=jnp.float32)
    inverse = jnp.power(jnp.float32(THETA), -2.0 * half / width)
    positions = length + jnp.arange(rows, dtype=jnp.int32)
    angles = positions.astype(jnp.float32)[:, None] * inverse[None, :]
    cosine = jnp.cos(angles)
    sine = jnp.sin(angles)
    cosine = jnp.concatenate([cosine, cosine], axis=1)
    sine = jnp.concatenate([-sine, sine], axis=1)
    owners = jnp.sum(jnp.where(served[:, :, None], page_owner[None], 0), axis=1)
    held = jnp.sum(jnp.where(served[:, :, None], page_slot[None], 0), axis=1)
    pages = jnp.arange(pages_max, dtype=jnp.int32)
    owned = owners == device
    rank = jnp.sum(
        jnp.where(pages[None, :, None] > pages[None, None, :], owned[:, None, :], False).astype(
            jnp.int32
        ),
        axis=2,
    )
    left = jnp.clip(lengths[:, None] - pages[None, :] * page_len, 0, page_len)
    choose = jnp.arange(per_owner, dtype=jnp.int32)
    picked = owned[:, None, :] & (rank[:, None, :] == choose[None, :, None])
    slot_pick = jnp.sum(jnp.where(picked, held[:, None, :], 0), axis=2)
    valid = jnp.sum(jnp.where(picked, left[:, None, :], 0), axis=2)
    return layer(
        groups,
        lax.axis_size("tp"),
        per_owner,
        (slot_pick, valid, cosine, sine),
        (norm_gain[None, :], mlp_gain[None, :]),
        tokens,
        (w_query, w_key, w_value, w_out, w_gate, w_up, w_down),
        kv_pool,
    )


def solution(mesh):
    in_specs = (
        P("dp", "tp"),
        P(),
        P(None, "tp"),
        P(None, "tp"),
        P(None, "tp"),
        P("tp", None),
        P(),
        P(None, "tp"),
        P(None, "tp"),
        P("tp", None),
        P("dp", None, "tp", None, None),
        P(),
        P(),
        P(),
        P(),
    )
    out_specs = (P("dp", "tp"), P("dp", "tp"))
    return jax.shard_map(shards, mesh=mesh, in_specs=in_specs, out_specs=out_specs, check_vma=False)
```

time: 200 us -> 142 us (0.71)
  Pallas kernels: 151 us -> 131 us
  between operations: 14.2 us -> 0.69 us
  matrix products: 11.3 us -> 0 us
  local copies, waits for them, and re-layouts: 9.59 us -> 4.91 us
  waiting for transfers between devices: 3.79 us -> 0 us
  other arithmetic: 8.76 us -> 5.46 us
    pallas_call x3 -> x1, Pallas kernels: 151 us -> 131 us  [layer(): pl.pallas_call(functools.partial(layer_kernel, (groups, ranks, kv_heads,...]
    dot_general x3 -> x0, matrix products: 11.3 us -> none  [the longest x1 6.82 us: shards(): jnp.dot(normed, w_query, preferred_element_type=jnp.float32)]
    gather x3 -> x0, local copies, waits for them, and re-layouts: 3.14 us -> none  [the longest x1 1.31 us: shards(): length_dest = jnp.take(prefix_len, serving)]
    all_gather x1 -> x0, waiting for transfers between devices: 3.11 us -> none  [shards(): gathered = lax.all_gather(tokens, 'tp', axis=1, tiled=True)]
    unnamed x16 -> x2, local copies, waits for them, and re-layouts: 4.17 us -> 3.55 us
  transfers between devices with their start and end apart: 1 -> 0, of which waited for: 1 -> 0; matrix products, arithmetic and copies ran while one was open for 5% -> 0% of each run, Pallas kernels for 0% -> 0%
where the time goes in v1:
time: 142 us
  Pallas kernels  131 us (92%)
  other arithmetic  5.46 us (4%)
  local copies, waits for them, and re-layouts  4.91 us (3%)
    pallas_call x1, Pallas kernels, layer(): pl.pallas_call(functools.partial(layer_kernel, (groups, ranks, kv_heads,...  131 us
    unnamed x2, local copies, waits for them, and re-layouts  3.55 us

profile of v1, /device:TPU:1, one launch (start us, length us, event | category | flops | bytes accessed | tf_op | source)
XLA Modules:
  0.0 141.6 jit_solution(11875173476489902092)
XLA Ops:
  0.6 0.9 select_reduce_fusion.4
  1.5 0.6 fusion.2
  2.1 0.6 add_convert_fusion
  2.8 0.7 iota_compare_fusion.2
  3.5 0.1 subtract_clamp_fusion
  3.6 0.8 select_reduce_fusion.1
  4.5 0.3 convert_reduce_fusion
  4.9 0.2 select_reduce_fusion.2
  5.1 0.7 copy.18.valid_ref
  5.8 0.7 copy.17.slot_ref
  6.4 0.3 fusion.1
  6.7 0.8 pad_maximum_fusion
  7.5 130.6 %layer.1 = (bf16[128,1024]{1,0:T(8,128)(2,1)}, bf16[128,2048]{1,0:T(8,128)(2,1)}) custom-call(s32[16,4]{1,0:T(8,128)} %copy.17.slot_ref, s32[16,4]{1,0:T(8,128)} %copy.18.valid_ref, f32[128,128]{1,0:T(8,128)} %get-tuple-element.9.cos_ref, f32[128,128]{1,0:T(8,128)} %get-tuple-element.10.sin_ref, f32[1,4096]{1,0:T(1,128)} %bitcast.2, f32[1,4096]{1,0:T(1,128)} %bitcast.3, ...), custom_call_target="tpu_custom_call" | custom-call | tf_op jit(solution)/shard_map/layer/pallas_call | solution.py:605
  138.1 1.7 %copy.21 = bf16[128,1024]{1,0:T(8,128)(2,1)} copy(bf16[128,1024]{1,0:T(8,128)(2,1)} %get-tuple-element.13) | data formatting | bytes 524288
  139.8 1.9 %copy.22 = bf16[128,2048]{1,0:T(8,128)(2,1)} copy(bf16[128,2048]{1,0:T(8,128)(2,1)} %get-tuple-element.14) | data formatting | bytes 1048576
  (4 shorter events, 0.0 us)

commit v2 on v1

--- a/solution.py
+++ b/solution.py
@@ -3,6 +3,7 @@
 
 import jax
 import jax.numpy as jnp
+import numpy as np
 from jax import lax
 from jax.experimental import pallas as pl
 from jax.experimental.pallas import tpu as pltpu
@@ -26,6 +27,49 @@
     return out
 
 
+TUNED = (
+    "C0", "I0.12", "I0.4", "I0.1", "C1", "I1.12", "I1.2", "I1.1", "I0.2", "I1.4", "F0.1",
+    "F1.1", "F0.12", "I1.8", "C2", "F0.2", "F0.4", "F1.12", "I0.8", "F1.4", "A1", "F0.13",
+    "F1.13", "F1.8", "F0.6", "F0.14", "F0.15", "F1.15", "F0.8", "F1.2", "A15", "R0.15", "F1.6",
+    "F1.9", "F1.14", "F0.5", "A12", "F1.5", "F0.9", "A13", "F1.10", "A4", "F1.11", "F0.10",
+    "R1.15", "M0.13", "A14", "A10", "R1.14", "R0.10", "F0.7", "F1.7", "A6", "A7", "M1.13",
+    "F0.11", "R0.14", "A5", "R1.7", "A9", "A11", "R1.11", "M1.12", "A2", "R0.11", "R1.10",
+    "R0.7", "N1.3", "M1.5", "M1.9", "M0.12", "F0.3", "R0.6", "N0.3", "M0.9", "F1.3", "A8", "A3",
+    "R0.3", "R1.6", "R1.3", "M1.8", "M0.8", "N0.2", "R1.2", "M0.5", "M1.4", "R0.2", "A0",
+    "N1.1", "N1.2", "M0.1", "M1.0", "M0.4", "M1.1", "N0.1", "N1.0", "M0.0", "N0.0",
+)
+
+
+def schedule(planes):
+    if planes == 4:
+        return [(word[0], [int(part) for part in word[1:].split(".")]) for word in TUNED]
+    tasks = []
+    for piece in range(2):
+        tasks.append(("C", [piece]))
+        tasks += [("I", [piece, key]) for key in (1, 2)]
+        tasks += [("I", [piece, 4 * j]) for j in range(1, planes)]
+    tasks.append(("C", [2]))
+    for key in range(4 * planes):
+        tasks += [("F", [piece, key]) for piece in range(2) if key]
+        tasks.append(("A", [key]))
+        tasks += [("R", [piece, key]) for piece in range(2) if key % 4 >= 2]
+    for j in reversed(range(planes)):
+        tasks += [("M", [piece, 4 * j + turn]) for turn in (1, 0) for piece in range(2)]
+    for j in reversed(range(planes)):
+        tasks += [("N", [piece, j]) for piece in range(2)]
+    return tasks
+
+
+def flipped(me, mask):
+    out = me
+    bit = 1
+    while bit <= mask:
+        if mask & bit:
+            out = out + (1 - 2 * lax.rem(lax.div(me, bit), 2)) * bit
+        bit *= 2
+    return out
+
+
 def merge_stats(left, right):
     shared = left.shape[0] // 2
     top = jnp.maximum(left[:shared], right[:shared])
@@ -37,12 +81,13 @@
 
 def layer_kernel(
     plan,
-    slot_ref,
-    valid_ref,
-    cos_ref,
-    sin_ref,
-    gain_ref,
-    mlp_gain_ref,
+    length_ref,
+    serving_ref,
+    owner_ref,
+    page_slot_ref,
+    inverse_ref,
+    norm_gain_ref,
+    mlp_norm_gain_ref,
     tokens_ref,
     wq_ref,
     wk_ref,
@@ -52,8 +97,8 @@
     wu_ref,
     wd_ref,
     kv_ref,
-    context_ref,
-    layer_ref,
+    context_out,
+    layer_out,
     ring,
     kv_buf,
     tok_all,
@@ -69,6 +114,23 @@
     hidden,
     mlp_part,
     mlp_box,
+    context_ref,
+    layer_ref,
+    cos_ref,
+    sin_ref,
+    inverse_buf,
+    gain_ref,
+    mlp_gain_ref,
+    owner_buf,
+    page_slot_buf,
+    owner_rows,
+    slot_rows,
+    length_rows,
+    picks,
+    picked,
+    small_sem,
+    picks_sem,
+    out_sem,
     ring_sem,
     kv_sem,
     tok_sem,
@@ -182,6 +244,20 @@
     own_columns = pl.ds(pl.multiple_of(rank * share, share), share)
     own_load = pltpu.make_async_copy(tokens_ref, tok_all.at[:, own_columns], tok_sem)
     own_load.start()
+    small = [
+        pltpu.make_async_copy(source, target, small_sem.at[i])
+        for i, (source, target) in enumerate(
+            (
+                (norm_gain_ref, gain_ref),
+                (inverse_ref, inverse_buf),
+                (owner_ref, owner_buf),
+                (page_slot_ref, page_slot_buf),
+                (mlp_norm_gain_ref, mlp_gain_ref),
+            )
+        )
+    ]
+    for copy in small:
+        copy.start()
     for tile in range(first_o):
         start_tile(tile)
 
@@ -216,6 +292,48 @@
         sends.append(copy)
     kv_load = pltpu.make_async_copy(kv_ref, kv_buf, kv_sem)
     kv_load.start()
+    for copy in small:
+        copy.wait()
+
+    length = length_ref[serving_ref[me]]
+    position = length + lax.broadcasted_iota(jnp.int32, (rows, width), 0)
+    angles = position.astype(jnp.float32) * inverse_buf[...]
+    lane = lax.broadcasted_iota(jnp.int32, (rows, width), 1)
+    cos_ref[...] = jnp.cos(angles)
+    sine = jnp.sin(angles)
+    sin_ref[...] = jnp.where(lane < width // 2, -sine, sine)
+
+    pages_max = owner_buf.shape[1]
+    span = owner_rows.shape[1]
+
+    def group_row(group, carry):
+        request = serving_ref[group]
+        here = pl.ds(group, 1)
+        owner_rows[here, 0:pages_max] = owner_buf[pl.ds(request, 1), :]
+        slot_rows[here, 0:pages_max] = page_slot_buf[pl.ds(request, 1), :]
+        length_rows[here, :] = jnp.full((1, span), length_ref[request], jnp.int32)
+        return carry
+
+    lax.fori_loop(0, groups, group_row, 0)
+    lane = lax.broadcasted_iota(jnp.int32, (groups, span), 1)
+    owned = ((owner_rows[...] == me) & (lane < pages_max)).astype(jnp.int32)
+    before = owned
+    shift = 1
+    while shift < span:
+        before = before + jnp.where(lane >= shift, pltpu.roll(before, shift, 1), 0)
+        shift *= 2
+    before = before - owned
+    left = jnp.clip(length_rows[...] - lane * page, 0, page)
+    table = jnp.zeros((groups, span), jnp.int32)
+    for k in range(per_owner):
+        chosen = (owned > 0) & (before == k)
+        for at, source in ((k, slot_rows[...]), (per_owner + k, left)):
+            value = jnp.sum(jnp.where(chosen, source, 0), axis=1, keepdims=True)
+            table = table + jnp.where(lane == at, value, 0)
+    picks[...] = table
+    picks_copy = pltpu.make_async_copy(picks, picked, picks_sem)
+    picks_copy.start()
+
     own_load.wait()
     for t in range(ranks - 1):
         came = lax.rem(rank + 2 * ranks - 1 - t, ranks)
@@ -256,51 +374,71 @@
             key = key - low + lax.div(low, 2) + 2 * lax.rem(low, 2)
         return xor(me, key, bits)
 
+    def block_at(piece, key):
+        low = key % 4
+        if piece % 2:
+            low = low // 2 + 2 * (low % 2)
+        return flipped(me, key - key % 4 + low)
+
     tiles_each = q_tiles // kv_heads
     per_tile = q_width // width
-    for piece in range(kv_heads):
-
-        def project(t, carry, piece=piece):
-            tile = piece * tiles_each + t
+
+    def project(piece):
+        tiles = [piece * tiles_each + t for t in range(tiles_each)]
+        for tile in tiles:
             q_copy(tile).wait()
+        for tile in tiles:
             values = jnp.dot(
-                normed[...],
-                ring[slot_of(tile), :, 0:q_width],
-                preferred_element_type=jnp.float32,
+                normed[...], ring[tile, :, 0:q_width], preferred_element_type=jnp.float32
             )
             for h in range(per_tile):
                 q_all[me, tile * per_tile + h] = rope(
                     values[:, h * width : (h + 1) * width]
                 ).astype(jnp.bfloat16)
-            return carry
-
-        lax.fori_loop(0, tiles_each, project, 0)
-        for link in range(2):
-            send_query(piece, me, hops[piece % 2][link], 1 + link)
-        for j in range(1, planes):
-            send_query(piece, me, xor(me, 4 * j, bits), 4 * j)
+
+    def send_own(piece, key):
+        target = hops[piece % 2][key - 1] if key < 4 else flipped(me, key)
+        send_query(piece, me, target, key)
+
+    def forward(piece, key):
+        block = block_at(piece, key)
+        landed = q_all.at[block, pl.ds(piece * shared, shared)]
+        pltpu.make_async_copy(landed, landed, q_recv.at[piece, key]).wait()
+        if key % 4 == 0:
+            send_query(piece, block, hops[piece % 2][0], key + 1)
+        if key % 4 < 2:
+            send_query(piece, block, hops[piece % 2][1], key + 2)
+
+    tasks = [
+        (kind, spec)
+        for kind, spec in schedule(planes)
+        if kind in "CA" or spec[0] < kv_heads
+    ]
+    marks = [tasks.index(("C", [at])) for at in range(3)]
+    for at in range(2):
+        if at < kv_heads:
+            project(at)
+        for kind, spec in tasks[marks[at] + 1 : marks[at + 1]]:
+            (send_own if kind == "I" else forward)(*spec)
+    tasks = tasks[marks[2] + 1 :]
 
     for i in range(k_tiles):
         k_copy(i).wait()
-        values = jnp.dot(
-            normed[...], ring[first_k + i, :, 0:k_width], preferred_element_type=jnp.float32
-        )
-        for h in range(k_width // width):
-            new_k[i * (k_width // width) + h] = rope(
-                values[:, h * width : (h + 1) * width]
-            ).astype(jnp.bfloat16)
+        v_copy(i).wait()
+    per_tile = k_width // width
     for i in range(k_tiles):
-        v_copy(i).wait()
-        values = jnp.dot(
-            normed[...], ring[first_v + i, :, 0:k_width], preferred_element_type=jnp.float32
-        )
-        for h in range(k_width // width):
-            new_v[i * (k_width // width) + h] = values[:, h * width : (h + 1) * width].astype(
-                jnp.bfloat16
+        for first, store, turn in ((first_k, new_k, rope), (first_v, new_v, lambda v: v)):
+            values = jnp.dot(
+                normed[...], ring[first + i, :, 0:k_width], preferred_element_type=jnp.float32
             )
+            for h in range(per_tile):
+                store[i * per_tile + h] = turn(values[:, h * width : (h + 1) * width]).astype(
+                    jnp.bfloat16
+                )
     for tile in range(first_o, slots + first_o):
         start_tile(tile)
     kv_load.wait()
+    picks_copy.wait()
 
     scale = LOG2E / math.sqrt(width)
 
@@ -358,47 +496,7 @@
             landed = target_box.at[piece, key]
             pltpu.make_async_copy(landed, landed, in_sem.at[piece, key]).wait()
 
-    def landed_query(piece, key, block):
-        landed = q_all.at[block, pl.ds(piece * shared, shared)]
-        pltpu.make_async_copy(landed, landed, q_recv.at[piece, key]).wait()
-
     row = lax.broadcasted_iota(jnp.int32, (page, 1), 0)
-
-    def one_key(key, carry):
-        turn = lax.rem(key, 4)
-        for piece in range(kv_heads):
-            block = block_of(piece, key)
-            near_to, far_to = hops[piece % 2]
-
-            @pl.when(key > 0)
-            def _():
-                landed_query(piece, key, block)
-
-                @pl.when(turn == 0)
-                def _():
-                    send_query(piece, block, near_to, key + 1)
-
-                @pl.when(turn < 2)
-                def _():
-                    send_query(piece, block, far_to, key + 2)
-
-            pages = [slot_ref[block, k] for k in range(per_owner)]
-            ok = jnp.concatenate([row < valid_ref[block, k] for k in range(per_owner)], axis=0)
-            keys = jnp.concatenate([kv_buf[p, 0, piece] for p in pages], axis=0)
-            values = jnp.concatenate([kv_buf[p, 1, piece] for p in pages], axis=0)
-            keep(
-                attend(keys, values, ok, block, piece),
-                part.at[block, piece],
-                stat.at[block, piece],
-            )
-
-            @pl.when(turn >= 2)
-            def _():
-                send_part(piece, block, far_to, key)
-
-        return carry
-
-    lax.fori_loop(0, groups, one_key, 0)
 
     def merge_into(piece, block, key):
         merged, mine, other = merge_stats(stat[block, piece], stat_box[piece, key])
@@ -409,33 +507,68 @@
             ).astype(jnp.bfloat16)
         stat[block, piece] = merged
 
-    def first_merges(index, carry):
-        base = 4 * (planes - 1 - index)
-        for turn in (1, 0):
-            for piece in range(kv_heads):
-                block = block_of(piece, base + turn)
-                landed_part(piece, base + turn + 2)
-                merge_into(piece, block, base + turn + 2)
-                if turn:
-                    send_part(piece, block, hops[piece % 2][0], base + 1)
+    def run_task(kind, piece, key):
+        near_to, far_to = hops[piece % 2]
+        if kind == "I":
+            send_own(piece, key)
+            return
+        if kind == "N":
+            block = block_at(piece, 4 * key)
+            landed_part(piece, 4 * key + 1)
+            merge_into(piece, block, 4 * key + 1)
+            if key:
+                send_part(piece, block, block, 4 * key)
+            return
+        block = block_at(piece, key)
+        if kind == "F":
+            forward(piece, key)
+        elif kind == "R":
+            send_part(piece, block, far_to, key)
+        elif kind == "M":
+            landed_part(piece, key + 2)
+            merge_into(piece, block, key + 2)
+            if key % 4 == 1:
+                send_part(piece, block, near_to, key)
+
+    before_turn = [[]]
+    order = []
+    for kind, spec in tasks:
+        if kind == "A":
+            order.append(spec[0])
+            before_turn.append([])
+        else:
+            before_turn[-1].append((kind, *spec))
+
+    def one_turn(turn, carry):
+        for at, todo in enumerate(before_turn[:-1]):
+            if todo:
+
+                @pl.when(turn == at)
+                def _():
+                    for task in todo:
+                        run_task(*task)
+
+        key = 0
+        for at, value in enumerate(order):
+            key = jnp.where(turn == at, value, key)
+        for piece in range(kv_heads):
+            block = block_of(piece, key)
+            pages = [picked[block, k] for k in range(per_owner)]
+            ok = jnp.concatenate(
+                [row < picked[block, per_owner + k] for k in range(per_owner)], axis=0
+            )
+            keys = jnp.concatenate([kv_buf[p, 0, piece] for p in pages], axis=0)
+            values = jnp.concatenate([kv_buf[p, 1, piece] for p in pages], axis=0)
+            keep(
+                attend(keys, values, ok, block, piece),
+                part.at[block, piece],
+                stat.at[block, piece],
+            )
         return carry
 
-    lax.fori_loop(0, planes, first_merges, 0)
-
-    def second_merges(index, carry):
-        base = 4 * (planes - 1 - index)
-        for piece in range(kv_heads):
-            block = block_of(piece, base)
-            landed_part(piece, base + 1)
-            merge_into(piece, block, base + 1)
-
-            @pl.when(base > 0)
-            def _():
-                send_part(piece, block, block, base)
-
-        return carry
-
-    lax.fori_loop(0, planes, second_merges, 0)
+    lax.fori_loop(0, groups, one_turn, 0)
+    for task in before_turn[-1]:
+        run_task(*task)
 
     for piece in range(kv_heads):
 
@@ -461,6 +594,8 @@
             total = done[0][shared + h : shared + h + 1]
             context_ref[:, lanes] = (done[1 + h] / total).T.astype(jnp.bfloat16)
 
+    context_copy = pltpu.make_async_copy(context_ref, context_out, out_sem.at[0])
+    context_copy.start()
     for i in range(o_tiles):
         out_wait(i)
         for s in range(o_stack):
@@ -490,59 +625,68 @@
 
     normalize(mlp_gain_ref)
 
-    def gate_step(i, carry):
-        gate_copy(i, 0).wait()
-        gate = jnp.dot(
-            normed[...],
-            ring[slot_of(first_g + 2 * i), :, 0:g_width],
-            preferred_element_type=jnp.float32,
-        )
-        gate_copy(i, 1).wait()
-        up = jnp.dot(
-            normed[...],
-            ring[slot_of(first_g + 2 * i + 1), :, 0:g_width],
-            preferred_element_type=jnp.float32,
-        )
-        columns = pl.ds(pl.multiple_of(i * g_width, g_width), g_width)
-        hidden[:, columns] = (gate / (1.0 + jnp.exp(-gate)) * up).astype(jnp.bfloat16)
-        later = i + slots // 2
-
-        @pl.when(later < g_tiles)
-        def _():
-            gate_copy(later, 0).start()
-            gate_copy(later, 1).start()
-
-        for which in range(2):
-            down = 2 * (later - g_tiles) + which
-
-            @pl.when((later >= g_tiles) & (down < d_tiles))
+    pairs = math.gcd(g_tiles, 2)
+
+    def gate_step(index, carry):
+        mine = [index * pairs + u for u in range(pairs)]
+        for i in mine:
+            gate_copy(i, 0).wait()
+            gate_copy(i, 1).wait()
+        for i in mine:
+            gate, up = [
+                jnp.dot(
+                    normed[...],
+                    ring[slot_of(first_g + 2 * i + which), :, 0:g_width],
+                    preferred_element_type=jnp.float32,
+                )
+                for which in range(2)
+            ]
+            columns = pl.ds(pl.multiple_of(i * g_width, g_width), g_width)
+            hidden[:, columns] = (gate / (1.0 + jnp.exp(-gate)) * up).astype(jnp.bfloat16)
+        for i in mine:
+            later = i + slots // 2
+
+            @pl.when(later < g_tiles)
             def _():
-                down_copy(down).start()
+                gate_copy(later, 0).start()
+                gate_copy(later, 1).start()
+
+            for which in range(2):
+                down = 2 * (later - g_tiles) + which
+
+                @pl.when((later >= g_tiles) & (down < d_tiles))
+                def _():
+                    down_copy(down).start()
 
         return carry
 
-    lax.fori_loop(0, g_tiles, gate_step, 0)
+    lax.fori_loop(0, g_tiles // pairs, gate_step, 0)
 
     per_target = d_tiles // ranks
+    fours = math.gcd(per_target, 4)
     for t in range(ranks):
 
         def down_step(index, carry, t=t):
-            i = index + t * per_target
-            down_copy(i).wait()
-            columns = pl.ds(pl.multiple_of(index * d_width, d_width), d_width)
-            mlp_part[t, :, columns] = jnp.dot(
-                hidden[...],
-                ring[slot_of(first_d + i), 0:units, 0:d_width],
-                preferred_element_type=jnp.float32,
-            ).astype(jnp.bfloat16)
-
-            @pl.when(i + slots < d_tiles)
-            def _():
-                down_copy(i + slots).start()
+            mine = [index * fours + u for u in range(fours)]
+            for at in mine:
+                down_copy(at + t * per_target).wait()
+            for at in mine:
+                columns = pl.ds(pl.multiple_of(at * d_width, d_width), d_width)
+                mlp_part[t, :, columns] = jnp.dot(
+                    hidden[...],
+                    ring[slot_of(first_d + at + t * per_target), 0:units, 0:d_width],
+                    preferred_element_type=jnp.float32,
+                ).astype(jnp.bfloat16)
+            for at in mine:
+                later = at + t * per_target + slots
+
+                @pl.when(later < d_tiles)
+                def _():
+                    down_copy(later).start()
 
             return carry
 
-        lax.fori_loop(0, per_target, down_step, 0)
+        lax.fori_loop(0, per_target // fours, down_step, 0)
         if t < ranks - 1:
             copy = to_peer(
                 mlp_part.at[t], mlp_box.at[t], mlp_send.at[t], mlp_recv.at[t], peers[t]
@@ -555,6 +699,8 @@
         mlp_sum = mlp_sum + mlp_box[t].astype(jnp.float32)
     layer_ref[...] = (tok_all[:, own_columns].astype(jnp.float32) + mlp_sum).astype(jnp.bfloat16)
 
+    layer_copy = pltpu.make_async_copy(layer_ref, layer_out, out_sem.at[1])
+    layer_copy.start()
     for copy in sends:
         copy.wait_send()
 
@@ -568,21 +714,43 @@
         return carry
 
     lax.fori_loop(1, groups, settle, 0)
-
-
-def layer(groups, ranks, per_owner, tables, gains, tokens, weights, kv_pool):
-    slot_pick, valid, cosine, sine = tables
+    context_copy.wait()
+    layer_copy.wait()
+
+
+def finish_kernel(context_ref, layer_ref, context_out, layer_out, buf_a, buf_b, sems):
+    pairs = ((context_ref, buf_a, context_out), (layer_ref, buf_b, layer_out))
+    for i, (source, buf, _) in enumerate(pairs):
+        pltpu.make_async_copy(source, buf, sems.at[i]).start()
+    for i, (source, buf, target) in enumerate(pairs):
+        pltpu.make_async_copy(source, buf, sems.at[i]).wait()
+        pltpu.make_async_copy(buf, target, sems.at[i]).start()
+    for i, (_, buf, target) in enumerate(pairs):
+        pltpu.make_async_copy(buf, target, sems.at[i]).wait()
+
+
+def layer(groups, ranks, small, gains, tokens, weights, kv_pool):
+    lengths, serving, owners, page_slots, inverse = small
     rows, share = tokens.shape
     model = share * ranks
     _, _, kv_heads, page, width = kv_pool.shape
+    pages_max = owners.shape[1]
+    per_owner = (pages_max + groups - 1) // groups
+    span = (pages_max + 127) // 128 * 128
     heads = weights[0].shape[1] // width
     units = weights[4].shape[1]
     shared = heads // kv_heads
     bf16 = jnp.bfloat16
+    f32 = jnp.float32
+    i32 = jnp.int32
     dma = pltpu.SemaphoreType.DMA
     vmem = pl.BlockSpec(memory_space=VMEM)
     smem = pl.BlockSpec(memory_space=pltpu.SMEM)
     hbm = pl.BlockSpec(memory_space=pl.ANY)
+    outs = (
+        jax.ShapeDtypeStruct((rows, heads * width), bf16),
+        jax.ShapeDtypeStruct((rows, share), bf16),
+    )
     buffers = [
         (kv_pool.shape, bf16),
         ((rows, model), bf16),
@@ -591,28 +759,42 @@
         ((kv_heads, rows, width), bf16),
         ((kv_heads, rows, width), bf16),
         ((groups, kv_heads, shared, width, rows), bf16),
-        ((groups, kv_heads, 2 * shared, rows), jnp.float32),
+        ((groups, kv_heads, 2 * shared, rows), f32),
         ((kv_heads, groups, shared, width, rows), bf16),
-        ((kv_heads, groups, 2 * shared, rows), jnp.float32),
+        ((kv_heads, groups, 2 * shared, rows), f32),
         ((ranks, rows, model), bf16),
         ((rows, units), bf16),
         ((ranks, rows, share), bf16),
         ((ranks, rows, share), bf16),
+        ((rows, heads * width), bf16),
+        ((rows, share), bf16),
+        ((rows, width), f32),
+        ((rows, width), f32),
+        ((1, width), f32),
+        ((1, model), f32),
+        ((1, model), f32),
+        (owners.shape, i32),
+        (owners.shape, i32),
+        ((groups, span), i32),
+        ((groups, span), i32),
+        ((groups, span), i32),
+        ((groups, span), i32),
     ]
     used = sum(math.prod(shape) * jnp.dtype(kind).itemsize for shape, kind in buffers)
-    used += 2 * rows * (heads * width + share) + 8 * rows * width + 64 * model + 2_500_000
+    used += 64 * model + 2_500_000
     slots = (VMEM_BUDGET - used) // (2 * model * TILE) // 2 * 2
-    return pl.pallas_call(
+    found = pl.pallas_call(
         functools.partial(layer_kernel, (groups, ranks, kv_heads, per_owner)),
-        out_shape=(
-            jax.ShapeDtypeStruct((rows, heads * width), bf16),
-            jax.ShapeDtypeStruct((rows, share), bf16),
-        ),
-        in_specs=[smem, smem, vmem, vmem, vmem, vmem] + [hbm] * 9,
-        out_specs=(vmem, vmem),
+        out_shape=outs,
+        in_specs=[smem, smem] + [hbm] * 14,
+        out_specs=(hbm, hbm),
         scratch_shapes=[VMEM((slots, model, TILE), bf16)]
         + [VMEM(shape, kind) for shape, kind in buffers]
         + [
+            pltpu.SMEM((groups, span), i32),
+            dma((5,)),
+            dma,
+            dma((2,)),
             dma((slots,)),
             dma,
             dma,
@@ -633,7 +815,15 @@
             collective_id=0, has_side_effects=True, vmem_limit_bytes=67_000_000
         ),
         name="layer",
-    )(slot_pick, valid, cosine, sine, *gains, tokens, *weights, kv_pool)
+    )(lengths, serving, owners, page_slots, inverse, *gains, tokens, *weights, kv_pool)
+    return pl.pallas_call(
+        finish_kernel,
+        out_shape=outs,
+        in_specs=[hbm, hbm],
+        out_specs=(hbm, hbm),
+        scratch_shapes=[VMEM(out.shape, out.dtype) for out in outs] + [dma((2,))],
+        name="finish",
+    )(*found)
 
 
 def shards(
@@ -653,45 +843,14 @@
     page_slot,
     serving,
 ):
-    groups = lax.axis_size("dp")
-    device = lax.axis_index("dp")
-    rows = tokens.shape[0]
-    pages_max = page_owner.shape[1]
-    per_owner = (pages_max + groups - 1) // groups
-    page_len = kv_pool.shape[3]
     width = kv_pool.shape[4]
-    ids = jnp.arange(groups, dtype=jnp.int32)
-    served = serving[:, None] == ids[None, :]
-    lengths = jnp.sum(jnp.where(served, prefix_len[None, :], 0), axis=1)
-    length = jnp.sum(jnp.where(ids == device, lengths, 0))
-    half = jnp.arange(width // 2, dtype=jnp.float32)
-    inverse = jnp.power(jnp.float32(THETA), -2.0 * half / width)
-    positions = length + jnp.arange(rows, dtype=jnp.int32)
-    angles = positions.astype(jnp.float32)[:, None] * inverse[None, :]
-    cosine = jnp.cos(angles)
-    sine = jnp.sin(angles)
-    cosine = jnp.concatenate([cosine, cosine], axis=1)
-    sine = jnp.concatenate([-sine, sine], axis=1)
-    owners = jnp.sum(jnp.where(served[:, :, None], page_owner[None], 0), axis=1)
-    held = jnp.sum(jnp.where(served[:, :, None], page_slot[None], 0), axis=1)
-    pages = jnp.arange(pages_max, dtype=jnp.int32)
-    owned = owners == device
-    rank = jnp.sum(
-        jnp.where(pages[None, :, None] > pages[None, None, :], owned[:, None, :], False).astype(
-            jnp.int32
-        ),
-        axis=2,
-    )
-    left = jnp.clip(lengths[:, None] - pages[None, :] * page_len, 0, page_len)
-    choose = jnp.arange(per_owner, dtype=jnp.int32)
-    picked = owned[:, None, :] & (rank[:, None, :] == choose[None, :, None])
-    slot_pick = jnp.sum(jnp.where(picked, held[:, None, :], 0), axis=2)
-    valid = jnp.sum(jnp.where(picked, left[:, None, :], 0), axis=2)
+    half = np.arange(width // 2)
+    inverse = (THETA ** (-2.0 * half / width)).astype(np.float32)
+    inverse = jnp.asarray(np.concatenate([inverse, inverse])[None, :])
     return layer(
-        groups,
+        lax.axis_size("dp"),
         lax.axis_size("tp"),
-        per_owner,
-        (slot_pick, valid, cosine, sine),
+        (prefix_len, serving, page_owner, page_slot, inverse),
         (norm_gain[None, :], mlp_gain[None, :]),
         tokens,
         (w_query, w_key, w_value, w_out, w_gate, w_up, w_down),

time: 142 us -> 113 us (0.80)
  Pallas kernels: 131 us -> 112 us
  other arithmetic: 5.46 us -> 0 us
  local copies, waits for them, and re-layouts: 4.91 us -> 0 us
    pallas_call x1, Pallas kernels: 131 us -> 110 us  [layer(): pl.pallas_call(functools.partial(layer_kernel, (groups, ranks, kv_heads,...]
    unnamed x2 -> x0, local copies, waits for them, and re-layouts: 3.55 us -> none
    reduce_sum x5 -> x0, other arithmetic: 2.91 us -> none  [the longest x1 0.85 us: shards(): lengths = jnp.sum(jnp.where(served, prefix_len[None, :], 0), axis=1)]
    pallas_call x0 -> x1, Pallas kernels: none -> 1.93 us  [layer(): pl.pallas_call(finish_kernel, out_shape=outs, in_specs=[hbm, hbm], out_sp...]
where the time goes in v2:
time: 113 us
  Pallas kernels  112 us (99%)
    pallas_call x1, Pallas kernels, layer(): pl.pallas_call(functools.partial(layer_kernel, (groups, ranks, kv_heads,...  110 us

profile of v2, /device:TPU:1, one launch (start us, length us, event | category | flops | bytes accessed | tf_op | source)
XLA Modules:
  0.0 112.5 jit_solution(1936864230167851941)
XLA Ops:
  0.6 110.0 %layer.1 = (bf16[128,1024]{1,0:T(8,128)(2,1)}, bf16[128,2048]{1,0:T(8,128)(2,1)}) custom-call(s32[16]{0:T(128)} %length_ref.1, s32[16]{0:T(128)} %serving_ref.1, s32[16,64]{1,0:T(8,128)} %owner_ref.1, s32[16,64]{1,0:T(8,128)} %page_slot_ref.1, f32[1,128]{1,0:T(1,128)} %constant.2.clone.inverse_ref, f32[1,4096]{1,0:T(1,128)} %bitcast.2, f32[1,4096]{1,0:T(1,128)} %bitcast.3, ...), custom_call_target="tpu_custom_call" | custom-call | tf_op jit(solution)/shard_map/layer/pallas_call | solution.py:786
  110.6 1.9 %finish.1 = (bf16[128,1024]{1,0:T(8,128)(2,1)}, bf16[128,2048]{1,0:T(8,128)(2,1)}) custom-call(bf16[128,1024]{1,0:T(8,128)(2,1)} %get-tuple-element.4.context_ref, bf16[128,2048]{1,0:T(8,128)(2,1)} %get-tuple-element.5.layer_ref), custom_call_target="tpu_custom_call" | custom-call | tf_op jit(solution)/shard_map/finish/pallas_call | solution.py:819

commit v3 on v2

--- a/solution.py
+++ b/solution.py
@@ -28,35 +28,45 @@
 
 
 TUNED = (
-    "C0", "I0.12", "I0.4", "I0.1", "C1", "I1.12", "I1.2", "I1.1", "I0.2", "I1.4", "F0.1",
-    "F1.1", "F0.12", "I1.8", "C2", "F0.2", "F0.4", "F1.12", "I0.8", "F1.4", "A1", "F0.13",
-    "F1.13", "F1.8", "F0.6", "F0.14", "F0.15", "F1.15", "F0.8", "F1.2", "A15", "R0.15", "F1.6",
-    "F1.9", "F1.14", "F0.5", "A12", "F1.5", "F0.9", "A13", "F1.10", "A4", "F1.11", "F0.10",
-    "R1.15", "M0.13", "A14", "A10", "R1.14", "R0.10", "F0.7", "F1.7", "A6", "A7", "M1.13",
-    "F0.11", "R0.14", "A5", "R1.7", "A9", "A11", "R1.11", "M1.12", "A2", "R0.11", "R1.10",
-    "R0.7", "N1.3", "M1.5", "M1.9", "M0.12", "F0.3", "R0.6", "N0.3", "M0.9", "F1.3", "A8", "A3",
-    "R0.3", "R1.6", "R1.3", "M1.8", "M0.8", "N0.2", "R1.2", "M0.5", "M1.4", "R0.2", "A0",
-    "N1.1", "N1.2", "M0.1", "M1.0", "M0.4", "M1.1", "N0.1", "N1.0", "M0.0", "N0.0",
+    "C0", "I0.2", "I0.1", "I2.12", "C1", "I1.2", "I3.4", "I1.1", "I0.12", "I1.4", "I2.1", "C2",
+    "I3.2", "F0.1", "I3.1", "I3.12", "F3.4", "F2.12", "I0.4", "F1.1", "I2.2", "I1.12", "F1.4",
+    "F0.12", "I2.4", "F0.4", "F3.12", "F3.1", "F1.12", "F3.6", "F2.1", "F2.4", "I0.8", "F0.13",
+    "A12", "F1.5", "F2.5", "I1.8", "F3.5", "F0.6", "F2.6", "F3.14", "F1.13", "F0.5", "F0.15",
+    "F1.14", "F0.14", "F2.14", "F1.6", "F3.13", "F2.13", "A6", "R2.6", "F0.8", "F3.7", "F1.7",
+    "I2.8", "I3.8", "F2.7", "R0.6", "A14", "R1.6", "F1.15", "A0", "R2.14", "F0.7", "F1.8",
+    "F1.2", "F2.15", "F3.15", "F0.2", "R1.14", "F2.9", "R3.14", "A15", "A13", "R1.15", "F2.2",
+    "F3.2", "F2.8", "A4", "R2.15", "R0.15", "A2", "M2.12", "F1.9", "M1.12", "R3.15", "F0.9",
+    "M3.12", "F0.3", "N2.12", "F3.8", "M2.13", "F3.9", "A8", "F2.3", "M1.13", "R3.2", "N2.13",
+    "N3.12", "A7", "M0.13", "R0.14", "R3.6", "A5", "M3.13", "F0.11", "N3.13", "N1.12", "F2.11",
+    "R3.7", "F3.11", "F1.3", "R2.7", "R0.7", "F0.10", "F1.10", "F3.10", "F2.10", "F1.11", "A11",
+    "R3.11", "R0.11", "A10", "R2.11", "F3.3", "R1.10", "M0.12", "M2.5", "N0.12", "R3.10", "A9",
+    "R1.11", "R2.10", "A3", "R1.7", "M3.5", "R0.2", "M0.9", "R0.10", "M1.4", "M2.4", "M0.4",
+    "M3.8", "M2.9", "M0.5", "N2.4", "N2.9", "M3.4", "R0.3", "N2.5", "R2.3", "R3.3", "M3.9",
+    "R1.3", "R1.2", "N3.8", "M1.8", "M2.8", "N3.5", "M1.9", "R2.2", "N2.8", "N3.4", "A1",
+    "N3.9", "M0.8", "N0.8", "M0.0", "M3.0", "M0.1", "M1.5", "N0.4", "N3.0", "M3.1", "N1.8",
+    "M2.1", "N3.1", "M1.1", "M2.0", "N1.4", "M1.0", "N2.0", "N2.1", "N0.0", "N1.0",
 )
 
 
 def schedule(planes):
     if planes == 4:
         return [(word[0], [int(part) for part in word[1:].split(".")]) for word in TUNED]
+    routes = range(4)
     tasks = []
     for piece in range(2):
         tasks.append(("C", [piece]))
-        tasks += [("I", [piece, key]) for key in (1, 2)]
-        tasks += [("I", [piece, 4 * j]) for j in range(1, planes)]
+        keys = [1, 2] + [4 * j for j in range(1, planes)]
+        tasks += [("I", [route, key]) for key in keys for route in (piece, piece + 2)]
     tasks.append(("C", [2]))
     for key in range(4 * planes):
-        tasks += [("F", [piece, key]) for piece in range(2) if key]
+        tasks += [("F", [route, key]) for route in routes if key]
         tasks.append(("A", [key]))
-        tasks += [("R", [piece, key]) for piece in range(2) if key % 4 >= 2]
+        tasks += [("R", [route, key]) for route in routes if key % 4 >= 2]
     for j in reversed(range(planes)):
-        tasks += [("M", [piece, 4 * j + turn]) for turn in (1, 0) for piece in range(2)]
+        tasks += [("M", [route, 4 * j + turn]) for turn in (1, 0) for route in routes]
     for j in reversed(range(planes)):
-        tasks += [("N", [piece, j]) for piece in range(2)]
+        tasks += [("N", [route, 4 * j]) for route in routes]
+        tasks += [("N", [route, 4 * j + 1]) for route in (2, 3)]
     return tasks
 
 
@@ -71,11 +81,10 @@
 
 
 def merge_stats(left, right):
-    shared = left.shape[0] // 2
-    top = jnp.maximum(left[:shared], right[:shared])
-    factor_left = jnp.exp2(left[:shared] - top)
-    factor_right = jnp.exp2(right[:shared] - top)
-    count = left[shared:] * factor_left + right[shared:] * factor_right
+    top = jnp.maximum(left[0:1], right[0:1])
+    factor_left = jnp.exp2(left[0:1] - top)
+    factor_right = jnp.exp2(right[0:1] - top)
+    count = left[1:2] * factor_left + right[1:2] * factor_right
     return jnp.concatenate([top, count], axis=0), factor_left, factor_right
 
 
@@ -271,6 +280,7 @@
     near = [x_to, y_to] + [xor(me, 4 * j, bits) for j in range(1, planes)]
     for other in near:
         pl.semaphore_signal(barrier, inc=1, device_id={"dp": other}, device_id_type=MESH)
+    own_load.wait()
     pl.semaphore_wait(barrier, len(near) + len(peers))
 
     def to_peer(source, target, send_sem, recv_sem, peer):
@@ -286,12 +296,15 @@
     sends = []
     for t, peer in enumerate(peers):
         copy = to_peer(
-            tokens_ref, tok_all.at[:, own_columns], tok_send.at[t], tok_recv.at[t], peer
+            tokens_ref,
+            tok_all.at[:, own_columns],
+            tok_send.at[t],
+            tok_recv.at[t],
+            peer,
         )
         copy.start()
         sends.append(copy)
     kv_load = pltpu.make_async_copy(kv_ref, kv_buf, kv_sem)
-    kv_load.start()
     for copy in small:
         copy.wait()
 
@@ -334,7 +347,6 @@
     picks_copy = pltpu.make_async_copy(picks, picked, picks_sem)
     picks_copy.start()
 
-    own_load.wait()
     for t in range(ranks - 1):
         came = lax.rem(rank + 2 * ranks - 1 - t, ranks)
         landed = tok_all.at[:, pl.ds(pl.multiple_of(came * share, share), share)]
@@ -357,13 +369,17 @@
     def rope(values):
         return values * cos_ref[...] + pltpu.roll(values, width // 2, 1) * sin_ref[...]
 
-    def send_query(piece, block, target, key):
-        cut = pl.ds(piece * shared, shared)
+    minor = shared // 4
+    parts_of = ((0, shared - minor), (shared - minor, minor))
+
+    def send_query(route, block, target, key):
+        start, size = parts_of[route // 2]
+        cut = pl.ds((route % 2) * shared + start, size)
         pltpu.make_async_remote_copy(
             src_ref=q_all.at[block, cut],
             dst_ref=q_all.at[block, cut],
-            send_sem=q_send.at[piece, key],
-            recv_sem=q_recv.at[piece, key],
+            send_sem=q_send.at[route, key],
+            recv_sem=q_recv.at[route, key],
             device_id={"dp": target},
             device_id_type=MESH,
         ).start()
@@ -396,28 +412,35 @@
                     values[:, h * width : (h + 1) * width]
                 ).astype(jnp.bfloat16)
 
-    def send_own(piece, key):
-        target = hops[piece % 2][key - 1] if key < 4 else flipped(me, key)
-        send_query(piece, me, target, key)
-
-    def forward(piece, key):
-        block = block_at(piece, key)
-        landed = q_all.at[block, pl.ds(piece * shared, shared)]
-        pltpu.make_async_copy(landed, landed, q_recv.at[piece, key]).wait()
-        if key % 4 == 0:
-            send_query(piece, block, hops[piece % 2][0], key + 1)
+    def send_own(route, key):
+        target = hops[route % 2][key - 1] if key < 4 else flipped(me, key)
+        send_query(route, me, target, key)
+
+    def forward(route, key):
+        block = block_at(route % 2, key)
+        near_to, far_to = hops[route % 2]
+        start, size = parts_of[route // 2]
+        landed = q_all.at[block, pl.ds((route % 2) * shared + start, size)]
+        pltpu.make_async_copy(landed, landed, q_recv.at[route, key]).wait()
+        if route >= 2 and key == 1:
+            for j in sorted(range(1, planes), key=lambda j: abs(j - 2) * 2 + j // 3):
+                send_query(route, block, flipped(me, 4 * j), 4 * j + 1)
+        if route < 2 and key % 4 == 0:
+            send_query(route, block, near_to, key + 1)
         if key % 4 < 2:
-            send_query(piece, block, hops[piece % 2][1], key + 2)
+            send_query(route, block, far_to, key + 2)
 
     tasks = [
         (kind, spec)
         for kind, spec in schedule(planes)
-        if kind in "CA" or spec[0] < kv_heads
+        if kind in "CA" or spec[0] % 2 < kv_heads
     ]
     marks = [tasks.index(("C", [at])) for at in range(3)]
     for at in range(2):
         if at < kv_heads:
             project(at)
+        if at == 0:
+            kv_load.start()
         for kind, spec in tasks[marks[at] + 1 : marks[at + 1]]:
             (send_own if kind == "I" else forward)(*spec)
     tasks = tasks[marks[2] + 1 :]
@@ -465,8 +488,8 @@
         for j in range(shared):
             lanes = slice(j * rows, (j + 1) * rows)
             part_to[j] = summed[:, lanes].astype(jnp.bfloat16)
-            stat_to[j : j + 1] = highest[:, lanes]
-            stat_to[shared + j : shared + j + 1] = count[:, lanes]
+            stat_to[j, 0:1] = highest[:, lanes]
+            stat_to[j, 1:2] = count[:, lanes]
 
     key_row = lax.broadcasted_iota(jnp.int32, (rows, shared * rows), 0)
     token = lax.rem(lax.broadcasted_iota(jnp.int32, (rows, shared * rows), 1), rows)
@@ -477,58 +500,64 @@
             stat_box.at[piece, 0],
         )
 
-    def send_part(piece, block, target, key):
+    def send_part(route, block, target, key):
+        piece = route % 2
+        cut = pl.ds(*parts_of[route // 2])
         for source, target_box, out_sem, in_sem in (
             (part, box, part_send, part_recv),
             (stat, stat_box, stat_send, stat_recv),
         ):
             pltpu.make_async_remote_copy(
-                src_ref=source.at[block, piece],
-                dst_ref=target_box.at[piece, key],
-                send_sem=out_sem.at[piece, key],
-                recv_sem=in_sem.at[piece, key],
+                src_ref=source.at[block, piece, cut],
+                dst_ref=target_box.at[piece, key, cut],
+                send_sem=out_sem.at[route, key],
+                recv_sem=in_sem.at[route, key],
                 device_id={"dp": target},
                 device_id_type=MESH,
             ).start()
 
-    def landed_part(piece, key):
+    def landed_part(route, key):
+        cut = pl.ds(*parts_of[route // 2])
         for target_box, in_sem in ((box, part_recv), (stat_box, stat_recv)):
-            landed = target_box.at[piece, key]
-            pltpu.make_async_copy(landed, landed, in_sem.at[piece, key]).wait()
+            landed = target_box.at[route % 2, key, cut]
+            pltpu.make_async_copy(landed, landed, in_sem.at[route, key]).wait()
 
     row = lax.broadcasted_iota(jnp.int32, (page, 1), 0)
 
-    def merge_into(piece, block, key):
-        merged, mine, other = merge_stats(stat[block, piece], stat_box[piece, key])
-        for j in range(shared):
+    def merge_into(route, block, key):
+        landed_part(route, key)
+        piece = route % 2
+        start, size = parts_of[route // 2]
+        for j in range(start, start + size):
+            merged, mine, other = merge_stats(stat[block, piece, j], stat_box[piece, key, j])
             part[block, piece, j] = (
-                part[block, piece, j].astype(jnp.float32) * mine[j : j + 1]
-                + box[piece, key, j].astype(jnp.float32) * other[j : j + 1]
+                part[block, piece, j].astype(jnp.float32) * mine
+                + box[piece, key, j].astype(jnp.float32) * other
             ).astype(jnp.bfloat16)
-        stat[block, piece] = merged
-
-    def run_task(kind, piece, key):
-        near_to, far_to = hops[piece % 2]
+            stat[block, piece, j] = merged
+
+    def run_task(kind, route, key):
+        near_to, far_to = hops[route % 2]
+        block = block_at(route % 2, key)
         if kind == "I":
-            send_own(piece, key)
-            return
-        if kind == "N":
-            block = block_at(piece, 4 * key)
-            landed_part(piece, 4 * key + 1)
-            merge_into(piece, block, 4 * key + 1)
-            if key:
-                send_part(piece, block, block, 4 * key)
-            return
-        block = block_at(piece, key)
-        if kind == "F":
-            forward(piece, key)
+            send_own(route, key)
+        elif kind == "F":
+            forward(route, key)
         elif kind == "R":
-            send_part(piece, block, far_to, key)
+            send_part(route, block, far_to, key)
         elif kind == "M":
-            landed_part(piece, key + 2)
-            merge_into(piece, block, key + 2)
-            if key % 4 == 1:
-                send_part(piece, block, near_to, key)
+            merge_into(route, block, key + 2)
+            if route < 2 and key % 4 == 1:
+                send_part(route, block, near_to, key)
+        elif kind == "N":
+            if route < 2:
+                merge_into(route, block, key + 1)
+            if key >= 4:
+                send_part(route, block, flipped(me, key - key % 4), key)
+            elif key == 1:
+                for j in range(1, planes):
+                    merge_into(route, block, 4 * j + 1)
+                send_part(route, block, near_to, 1)
 
     before_turn = [[]]
     order = []
@@ -572,27 +601,29 @@
 
     for piece in range(kv_heads):
 
-        def home_merge(j, carry, piece=piece):
+        def fold(held, total, key, h):
+            merged, mine, other = merge_stats(held, stat_box[piece, key, h])
+            return merged, total * mine + box[piece, key, h].astype(jnp.float32) * other
+
+        def home_merge(j, carry, piece=piece, fold=fold):
             @pl.when(j > 0)
             def _():
                 landed_part(piece, 4 * j)
-
-            merged, mine, other = merge_stats(carry[0], stat_box[piece, 4 * j])
-            sums = tuple(
-                carry[1 + h] * mine[h : h + 1]
-                + box[piece, 4 * j, h].astype(jnp.float32) * other[h : h + 1]
-                for h in range(shared)
-            )
-            return (merged,) + sums
-
-        start = (stat[me, piece],) + tuple(
-            part[me, piece, h].astype(jnp.float32) for h in range(shared)
-        )
-        done = lax.fori_loop(0, planes, home_merge, start)
+                landed_part(piece + 2, 4 * j)
+
+            folded = [fold(carry[2 * h], carry[2 * h + 1], 4 * j, h) for h in range(shared)]
+            return tuple(item for pair in folded for item in pair)
+
+        start = []
+        for h in range(shared):
+            start += [stat[me, piece, h], part[me, piece, h].astype(jnp.float32)]
+        done = list(lax.fori_loop(0, planes, home_merge, tuple(start)))
+        landed_part(piece + 2, 1)
+        for h in range(shared - minor, shared):
+            done[2 * h : 2 * h + 2] = fold(done[2 * h], done[2 * h + 1], 1, h)
         for h in range(shared):
             lanes = slice((piece * shared + h) * width, (piece * shared + h + 1) * width)
-            total = done[0][shared + h : shared + h + 1]
-            context_ref[:, lanes] = (done[1 + h] / total).T.astype(jnp.bfloat16)
+            context_ref[:, lanes] = (done[2 * h + 1] / done[2 * h][1:2]).T.astype(jnp.bfloat16)
 
     context_copy = pltpu.make_async_copy(context_ref, context_out, out_sem.at[0])
     context_copy.start()
@@ -705,12 +736,16 @@
         copy.wait_send()
 
     def settle(key, carry):
-        for piece in range(kv_heads):
-            sent = q_all.at[0, pl.ds(piece * shared, shared)]
-            pltpu.make_async_copy(sent, sent, q_send.at[piece, key]).wait()
+        for route in range(4):
+            piece = route % 2
+            if piece >= kv_heads:
+                continue
+            start, size = parts_of[route // 2]
+            sent = q_all.at[0, pl.ds(piece * shared + start, size)]
+            pltpu.make_async_copy(sent, sent, q_send.at[route, key]).wait()
             for source, out_sem in ((part, part_send), (stat, stat_send)):
-                sent = source.at[0, piece]
-                pltpu.make_async_copy(sent, sent, out_sem.at[piece, key]).wait()
+                sent = source.at[0, piece, pl.ds(start, size)]
+                pltpu.make_async_copy(sent, sent, out_sem.at[route, key]).wait()
         return carry
 
     lax.fori_loop(1, groups, settle, 0)
@@ -759,9 +794,9 @@
         ((kv_heads, rows, width), bf16),
         ((kv_heads, rows, width), bf16),
         ((groups, kv_heads, shared, width, rows), bf16),
-        ((groups, kv_heads, 2 * shared, rows), f32),
+        ((groups, kv_heads, shared, 2, rows), f32),
         ((kv_heads, groups, shared, width, rows), bf16),
-        ((kv_heads, groups, 2 * shared, rows), f32),
+        ((kv_heads, groups, shared, 2, rows), f32),
         ((ranks, rows, model), bf16),
         ((rows, units), bf16),
         ((ranks, rows, share), bf16),
@@ -800,12 +835,12 @@
             dma,
             dma((ranks,)),
             dma((ranks,)),
-            dma((kv_heads, groups)),
-            dma((kv_heads, groups)),
-            dma((kv_heads, groups)),
-            dma((kv_heads, groups)),
-            dma((kv_heads, groups)),
-            dma((kv_heads, groups)),
+            dma((4, groups)),
+            dma((4, groups)),
+            dma((4, groups)),
+            dma((4, groups)),
+            dma((4, groups)),
+            dma((4, groups)),
             dma((ranks, 8)),
             dma((ranks, 8)),
             dma((ranks,)),

time: 113 us -> 112 us (level)
  no operation moved by 1% of the time
where the time goes in v3:
time: 112 us
  Pallas kernels  111 us (99%)
    pallas_call x1, Pallas kernels, layer(): pl.pallas_call(functools.partial(layer_kernel, (groups, ranks, kv_heads,...  109 us

profile of v3, /device:TPU:1, one launch (start us, length us, event | category | flops | bytes accessed | tf_op | source)
XLA Modules:
  0.0 111.8 jit_solution(2904596951509064710)
XLA Ops:
  0.6 109.2 %layer.1 = (bf16[128,1024]{1,0:T(8,128)(2,1)}, bf16[128,2048]{1,0:T(8,128)(2,1)}) custom-call(s32[16]{0:T(128)} %length_ref.1, s32[16]{0:T(128)} %serving_ref.1, s32[16,64]{1,0:T(8,128)} %owner_ref.1, s32[16,64]{1,0:T(8,128)} %page_slot_ref.1, f32[1,128]{1,0:T(1,128)} %constant.2.clone.inverse_ref, f32[1,4096]{1,0:T(1,128)} %bitcast.2, f32[1,4096]{1,0:T(1,128)} %bitcast.3, ...), custom_call_target="tpu_custom_call" | custom-call | tf_op jit(solution)/shard_map/layer/pallas_call | solution.py:821
  109.8 1.9 %finish.1 = (bf16[128,1024]{1,0:T(8,128)(2,1)}, bf16[128,2048]{1,0:T(8,128)(2,1)}) custom-call(bf16[128,1024]{1,0:T(8,128)(2,1)} %get-tuple-element.4.context_ref, bf16[128,2048]{1,0:T(8,128)(2,1)} %get-tuple-element.5.layer_ref), custom_call_target="tpu_custom_call" | custom-call | tf_op jit(solution)/shard_map/finish/pallas_call | solution.py:854
